TPU v7x, 32 devices: a whole 2x2x4 slice. The times are simulated.
32 devices in a mesh: blk: 16 (over z, x, core), cuts: 2 (over y).
Axes of the slice: x: 2, y: 2, z: 4, core: 2. Of those that a mesh axis runs over, the one named last changes fastest.
Arguments:
- left_env: bfloat16 [2048, 8, 2048], P('blk', 'cuts'), may hold values from -4 to 4
- right_env: bfloat16 [2048, 8, 2048], P('blk', 'cuts'), may hold values from -4 to 4
- left_core: float32 [8, 8, 2, 2], replicated, may hold values from -1.5 to 1.5
- right_core: float32 [8, 8, 2, 2], replicated, may hold values from -1.5 to 1.5
- slot_bond: int32 [8], replicated, may hold values from 0 to 7, each once
- krylov_basis: float32 [8, 2048, 4, 2048], P(None, 'blk', None, 'cuts'), may hold values from -30 to 30
- beta_prev: float32 [], replicated, may hold values from 0.3 to 1.2
Outputs:
- next_vector: float32 [2048, 4, 2048], P('blk', None, 'cuts')
- alpha_values: float32 [1], replicated
- beta_values: float32 [1], replicated
Inputs may be any that keep to these rules, and one draw needn't show every extreme that they name: `slot_bond`: a permutation of the 8 bond values.
All inputs are finite; a program needn't handle non-finite values.
Results may differ from a plain program's by a relative error of at most 0.00073.
The roundings to bfloat16 on the way count: a program that leaves them out, or rounds other values in their place, can miss the bound.
Values may be sent and summed in bfloat16 or wider, within the bound.
A program may use at most 192 MiB of HBM per device.

v0:
```python
import functools

import jax
import jax.numpy as jnp
from jax import lax
from jax.experimental import pallas as pl
from jax.experimental.pallas import tpu as pltpu
from jax.sharding import PartitionSpec as P

VMEM_BYTES = 60 * 1024 * 1024


def params():
    return pltpu.CompilerParams(vmem_limit_bytes=VMEM_BYTES)


def tile_of(size, most):
    return most if size % most == 0 else size


def build_table(left_core, right_core, slot_bond):
    bond_width = left_core.shape[0]
    phys_dim = left_core.shape[2]
    chosen = (slot_bond[:, None] == jnp.arange(bond_width, dtype=jnp.int32)[None, :]).astype(
        jnp.float32
    )
    picked = jnp.einsum("kw,wxac->kxac", chosen, left_core, precision=lax.Precision.HIGHEST)
    table = jnp.einsum("kxac,xybd->kyabcd", picked, right_core, precision=lax.Precision.HIGHEST)
    return table.reshape(bond_width, bond_width, phys_dim * phys_dim, phys_dim * phys_dim)


def mix_kernel(mix_ref, left_ref, cur_ref, out_ref, proj):
    slots, rows, depth = left_ref.shape
    pairs = cur_ref.shape[0]
    bonds = out_ref.shape[0]
    cols = cur_ref.shape[2]

    @pl.loop(0, pairs)
    def _(q):
        proj[q] = jnp.dot(
            left_ref[...].reshape(slots * rows, depth),
            cur_ref[q],
            preferred_element_type=jnp.float32,
        ).reshape(slots, rows, cols)

    @pl.loop(0, rows // 16)
    def _(g):
        mixed = []
        for h in range(2):
            at = pl.ds(pl.multiple_of(g * 16 + h * 8, 8), 8)
            stacked = jnp.concatenate(
                [proj[q, k, at, :] for k in range(slots) for q in range(pairs)], axis=0
            )
            mixed.append(
                jnp.dot(
                    mix_ref[...],
                    stacked,
                    precision=lax.Precision.HIGHEST,
                    preferred_element_type=jnp.float32,
                )
            )
        at = pl.ds(pl.multiple_of(g * 16, 16), 16)
        for y in range(bonds):
            for p in range(pairs):
                i = (y * pairs + p) * 8
                out_ref[y, p, at, :] = jnp.concatenate(
                    [m[i : i + 8] for m in mixed], axis=0
                ).astype(out_ref.dtype)


def mixed_left_of(table, left_k, cur_full):
    slots, rows, depth = left_k.shape
    pairs, _, cols = cur_full.shape
    bonds = table.shape[1]
    tb = tile_of(cols, 256)
    square = table.transpose(1, 2, 0, 3).reshape(bonds * pairs, slots * pairs)
    mix = jnp.kron(square, jnp.eye(8, dtype=jnp.float32))
    return pl.pallas_call(
        mix_kernel,
        grid=(cols // tb,),
        in_specs=[
            pl.BlockSpec(mix.shape, lambda i: (0, 0)),
            pl.BlockSpec((slots, rows, depth), lambda i: (0, 0, 0)),
            pl.BlockSpec((pairs, depth, tb), lambda i: (0, 0, i)),
        ],
        out_specs=pl.BlockSpec((bonds, pairs, rows, tb), lambda i: (0, 0, 0, i)),
        out_shape=jax.ShapeDtypeStruct((bonds, pairs, rows, cols), jnp.bfloat16),
        scratch_shapes=[pltpu.VMEM((pairs, slots, rows, tb), jnp.float32)],
        compiler_params=params(),
        cost_estimate=pl.CostEstimate(
            flops=2 * slots * rows * depth * pairs * cols,
            bytes_accessed=2 * (left_k.size + cur_full.size + bonds * pairs * rows * cols),
            transcendentals=0,
        ),
    )(mix, left_k, cur_full)


def image_kernel(start_ref, mixed_ref, right_ref, out_ref):
    bonds = mixed_ref.shape[0]
    out_ref[...] = jnp.zeros_like(out_ref)

    @pl.loop(0, bonds)
    def _(y):
        out_ref[...] += lax.dot_general(
            mixed_ref[y],
            right_ref[y],
            (((1,), (1,)), ((), ())),
            preferred_element_type=jnp.float32,
        )


def image_part(mixed, right_full, start, count):
    bonds, lines, cols = mixed.shape
    tb = tile_of(count, 256)
    return pl.pallas_call(
        image_kernel,
        grid_spec=pltpu.PrefetchScalarGridSpec(
            num_scalar_prefetch=1,
            grid=(count // tb,),
            in_specs=[
                pl.BlockSpec((bonds, lines, cols), lambda i, s: (0, 0, 0)),
                pl.BlockSpec((bonds, tb, cols), lambda i, s: (0, s[0] + i, 0)),
            ],
            out_specs=pl.BlockSpec((lines, tb), lambda i, s: (0, i)),
        ),
        out_shape=jax.ShapeDtypeStruct((lines, count), jnp.float32),
        compiler_params=params(),
        cost_estimate=pl.CostEstimate(
            flops=2 * bonds * lines * cols * count,
            bytes_accessed=2 * (mixed.size + bonds * count * cols),
            transcendentals=0,
        ),
    )((start // tb).reshape(1).astype(jnp.int32), mixed, right_full)


def gram_kernel(basis_ref, out_ref):
    basis_count, rows, pairs, cols = basis_ref.shape
    chunk = 4
    lanes = cols // 128

    @pl.when(pl.program_id(0) == 0)
    def _():
        out_ref[...] = jnp.zeros_like(out_ref)

    @pl.loop(0, rows // chunk)
    def _(r):
        for c in range(lanes):
            vecs = [
                basis_ref[j, pl.ds(r * chunk, chunk), :, c * 128 : (c + 1) * 128]
                for j in range(basis_count)
            ]
            i = 0
            for j in range(basis_count):
                for k in range(j, basis_count):
                    out_ref[i] += jnp.sum(vecs[j] * vecs[k], axis=0)
                    i += 1


def gram_of(basis):
    basis_count, rows, pairs, cols = basis.shape
    count = basis_count * (basis_count + 1) // 2
    ta = tile_of(rows, 16)
    sums = pl.pallas_call(
        gram_kernel,
        grid=(rows // ta,),
        in_specs=[pl.BlockSpec((basis_count, ta, pairs, cols), lambda i: (0, i, 0, 0))],
        out_specs=pl.BlockSpec((count, pairs, 128), lambda i: (0, 0, 0)),
        out_shape=jax.ShapeDtypeStruct((count, pairs, 128), jnp.float32),
        compiler_params=params(),
        cost_estimate=pl.CostEstimate(
            flops=2 * count * rows * pairs * cols,
            bytes_accessed=4 * basis.size,
            transcendentals=0,
        ),
    )(basis)
    return jnp.sum(sums, axis=(1, 2))


def dots_kernel(basis_ref, image_ref, out_ref):
    basis_count, rows, pairs, cols = basis_ref.shape

    @pl.when(pl.program_id(0) == 0)
    def _():
        out_ref[...] = jnp.zeros_like(out_ref)

    for c in range(cols // 128):
        at = slice(c * 128, (c + 1) * 128)
        image = image_ref[:, :, at]
        for j in range(basis_count):
            out_ref[j] += jnp.sum(basis_ref[j, :, :, at] * image, axis=0)
        out_ref[basis_count] += jnp.sum(image * image, axis=0)


def dots_of(basis, image):
    basis_count, rows, pairs, cols = basis.shape
    ta = tile_of(rows, 16)
    sums = pl.pallas_call(
        dots_kernel,
        grid=(rows // ta,),
        in_specs=[
            pl.BlockSpec((basis_count, ta, pairs, cols), lambda i: (0, i, 0, 0)),
            pl.BlockSpec((ta, pairs, cols), lambda i: (i, 0, 0)),
        ],
        out_specs=pl.BlockSpec((basis_count + 1, pairs, 128), lambda i: (0, 0, 0)),
        out_shape=jax.ShapeDtypeStruct((basis_count + 1, pairs, 128), jnp.float32),
        compiler_params=params(),
    )(basis, image)
    return jnp.sum(sums, axis=(1, 2))


def final_kernel(coef_ref, basis_ref, image_ref, out_ref):
    basis_count = basis_ref.shape[0]
    total = image_ref[...]
    for j in range(basis_count):
        total = total - coef_ref[j] * basis_ref[j]
    out_ref[...] = total * coef_ref[basis_count]


def final_of(coefs, basis, image):
    basis_count, rows, pairs, cols = basis.shape
    ta = tile_of(rows, 16)
    return pl.pallas_call(
        final_kernel,
        grid=(rows // ta,),
        in_specs=[
            pl.BlockSpec(memory_space=pltpu.SMEM),
            pl.BlockSpec((basis_count, ta, pairs, cols), lambda i: (0, i, 0, 0)),
            pl.BlockSpec((ta, pairs, cols), lambda i: (i, 0, 0)),
        ],
        out_specs=pl.BlockSpec((ta, pairs, cols), lambda i: (i, 0, 0)),
        out_shape=jax.ShapeDtypeStruct((rows, pairs, cols), jnp.float32),
        compiler_params=params(),
    )(coefs, basis, image)


def on_device(
    cuts, left_env, right_env, left_core, right_core, slot_bond, krylov_basis, beta_prev
):
    bond_width = left_core.shape[0]
    pair_count = left_core.shape[2] * left_core.shape[2]
    basis_count, row_count, _, col_count = krylov_basis.shape
    full_width = left_env.shape[2]
    entries = float(full_width * pair_count * full_width)
    table = build_table(left_core, right_core, slot_bond)
    me = lax.axis_index("cuts")
    swap = [(0, 1), (1, 0)]

    current = krylov_basis[basis_count - 1].astype(jnp.bfloat16).transpose(1, 0, 2)
    left_t = left_env.transpose(1, 0, 2)
    right_t = right_env.transpose(1, 0, 2)
    if cuts == 2:
        half = left_t.shape[0]
        theirs = lax.dynamic_slice_in_dim(right_t, (1 - me) * col_count, col_count, 2)
        mine = lax.dynamic_slice_in_dim(right_t, me * col_count, col_count, 2)
        right_k = jnp.concatenate([mine, lax.ppermute(theirs, "cuts", swap)], axis=0)
        left_k = jnp.concatenate([left_t, lax.ppermute(left_t, "cuts", swap)], axis=0)
        turned = jnp.roll(jnp.roll(table, -half, axis=0), -half, axis=1)
        table = jnp.where(me == 0, table, turned)
    else:
        left_k = lax.all_gather(left_t, "cuts", axis=0, tiled=True)
        right_k = lax.all_to_all(right_t, "cuts", split_axis=2, concat_axis=0, tiled=True)
    cur_full = lax.all_gather(current, "blk", axis=1, tiled=True)
    right_full = lax.all_gather(right_k, "blk", axis=1, tiled=True)
    gram = gram_of(krylov_basis)

    mixed = mixed_left_of(table, left_k, cur_full)
    mixed = mixed.reshape(bond_width, pair_count * row_count, col_count)
    if cuts == 2:
        away = image_part(mixed, right_full, (1 - me) * col_count, col_count)
        away = lax.ppermute(away, "cuts", swap)
        here = image_part(mixed, right_full, me * col_count, col_count)
        image = here + away
    else:
        image = image_part(mixed, right_full, jnp.int32(0), full_width)
        image = lax.psum_scatter(image, "cuts", scatter_dimension=1, tiled=True)
    image = image.reshape(pair_count, row_count, col_count).transpose(1, 0, 2)

    sums = lax.psum(jnp.concatenate([gram, dots_of(krylov_basis, image)]), ("blk", "cuts"))
    sums = sums / entries
    count = basis_count * (basis_count + 1) // 2
    where = []
    for j in range(basis_count):
        for k in range(basis_count):
            low, high = min(j, k), max(j, k)
            where.append(low * basis_count - low * (low - 1) // 2 + high - low)
    gram_matrix = sums[jnp.array(where)].reshape(basis_count, basis_count)
    inner_prods = sums[count : count + basis_count]
    image_square = sums[count + basis_count]
    last, prior = basis_count - 1, basis_count - 2
    alpha_now = inner_prods[last]
    ortho_coeffs = (
        inner_prods - alpha_now * gram_matrix[:, last] - beta_prev * gram_matrix[:, prior]
    )
    first_square = (
        image_square
        - 2.0 * alpha_now * inner_prods[last]
        - 2.0 * beta_prev * inner_prods[prior]
        + alpha_now * alpha_now * gram_matrix[last, last]
        + 2.0 * alpha_now * beta_prev * gram_matrix[last, prior]
        + beta_prev * beta_prev * gram_matrix[prior, prior]
    )
    square_mean = (
        first_square
        - 2.0 * jnp.sum(ortho_coeffs * ortho_coeffs)
        + jnp.sum(ortho_coeffs[:, None] * gram_matrix * ortho_coeffs[None, :])
    )
    beta_new = jnp.sqrt(square_mean + 1e-06)
    index = jnp.arange(basis_count)
    coefs = (
        ortho_coeffs
        + jnp.where(index == last, alpha_now, 0.0)
        + jnp.where(index == prior, beta_prev, 0.0)
    )
    coefs = jnp.concatenate([coefs, (1.0 / beta_new)[None]])
    next_vector = final_of(coefs, krylov_basis, image)
    return (next_vector, alpha_now[None], beta_new[None])


def solution(mesh):
    in_specs = (
        P("blk", "cuts", None),
        P("blk", "cuts", None),
        P(),
        P(),
        P(),
        P(None, "blk", None, "cuts"),
        P(),
    )
    out_specs = (P("blk", None, "cuts"), P(), P())
    return jax.shard_map(
        functools.partial(on_device, mesh.shape["cuts"]),
        mesh=mesh,
        in_specs=in_specs,
        out_specs=out_specs,
        check_vma=False,
    )
```

profile of v0, /device:TPU:0, one launch (start us, length us, event | category | flops | bytes accessed | tf_op | source)
XLA Modules:
  0.0 463.4 jit_solution(4286294273900218205)
XLA Ops:
  7.2 2.1 slice.78
  9.3 1.3 copy.50
  12.6 3.1 collective-permute-start.1
  16.0 22.8 %collective-permute-done.1 = bf16[4,128,1024]{2,1,0:T(8,128)(2,1)S(1)} collective-permute-done((bf16[4,128,1024]{2,1,0:T(8,128)(2,1)S(1)}, bf16[4,128,1024]{2,1,0:T(8,128)(2,1)S(1)}, u32[]{:S(2)}, u32[]{:S(2)}) %collective-permute-start.1) | collective-permute-done | bytes 1048608 | tf_op jit(solution)/shard_map/ppermute | solution.py:255
  38.8 1.5 pad_maximum_fusion.1
  40.4 2.8 copy.49
  43.1 1.8 collective-permute-start
  46.1 2.6 broadcast_multiply_fusion
  48.7 4.7 %mul.122.mix_ref = f32[256,256]{1,0:T(8,128)} reshape(f32[32,8,32,8]{3,2,1,0:T(8,128)} %broadcast_multiply_fusion) | data formatting | bytes 524288 | tf_op jit(solution)/shard_map/jit(kron)/mul | solution.py:77
  53.4 36.8 %collective-permute-done = bf16[4,128,2048]{2,1,0:T(8,128)(2,1)} collective-permute-done((bf16[4,128,2048]{2,1,0:T(8,128)(2,1)S(1)}, bf16[4,128,2048]{2,1,0:T(8,128)(2,1)}, u32[]{:S(2)}, u32[]{:S(2)}) %collective-permute-start) | collective-permute-done | bytes 2097184 | tf_op jit(solution)/shard_map/ppermute | solution.py:256
  90.2 3.9 pad_maximum_fusion.left_ref
  94.1 45.9 %all-gather.3.cloned.1.call-done.cur_ref = bf16[4,2048,1024]{2,1,0:T(8,128)(2,1)} async-done(((bf16[4,128,1024]{2,1,0:T(8,128)(2,1)}), bf16[4,2048,1024]{2,1,0:T(8,128)(2,1)}) %all-gather.3.cloned.1.call-update) | async-done | bytes 16777232 | tf_op jit(solution)/shard_map/all_gather | solution.py:262
  140.0 44.8 %shard_map.104 = bf16[8,4,128,1024]{3,2,1,0:T(8,128)(2,1)} custom-call(f32[256,256]{1,0:T(8,128)} %mul.122.mix_ref, bf16[8,128,2048]{2,1,0:T(8,128)(2,1)} %pad_maximum_fusion.left_ref, bf16[4,2048,1024]{2,1,0:T(8,128)(2,1)} %all-gather.3.cloned.1.call-done.cur_ref), custom_call_target="tpu_custom_call" | custom-call | flops 17179869184 | bytes 29360128 | tf_op jit(solution)/shard_map/pallas_call | solution.py:78
  184.8 123.5 %all-gather.5.cloned.1.call-done.right_ref = bf16[8,2048,1024]{2,1,0:T(8,128)(2,1)} async-done(((bf16[8,128,1024]{2,1,0:T(8,128)(2,1)}), bf16[8,2048,1024]{2,1,0:T(8,128)(2,1)}) %all-gather.5.cloned.1.call-update) | async-done | bytes 33554448 | tf_op jit(solution)/shard_map/all_gather | solution.py:263
  308.4 20.9 %shard_map.106 = f32[512,1024]{1,0:T(8,128)} custom-call(s32[1]{0:T(128)} %bitcast.17.start_ref, bf16[8,512,1024]{2,1,0:T(8,128)(2,1)} %bitcast.52, bf16[8,2048,1024]{2,1,0:T(8,128)(2,1)} %all-gather.5.cloned.1.call-done.right_ref), custom_call_target="tpu_custom_call" | custom-call | flops 8589934592 | bytes 25165824 | tf_op jit(solution)/shard_map/pallas_call | solution.py:115
  329.3 1.5 collective-permute-start.2
  331.4 17.4 %shard_map.103 = f32[36,4,128]{2,1,0:T(4,128)} custom-call(f32[8,128,4,1024]{3,2,1,0:T(4,128)} %basis_ref.5), custom_call_target="tpu_custom_call" | custom-call | flops 37748736 | bytes 16777216 | tf_op jit(solution)/shard_map/pallas_call | solution.py:163
  350.1 20.9 %shard_map.105 = f32[512,1024]{1,0:T(8,128)} custom-call(s32[1]{0:T(128)} %bitcast.start_ref, bf16[8,512,1024]{2,1,0:T(8,128)(2,1)} %bitcast.53, bf16[8,2048,1024]{2,1,0:T(8,128)(2,1)} %all-gather.5.cloned.1.call-done.right_ref), custom_call_target="tpu_custom_call" | custom-call | flops 8589934592 | bytes 25165824 | tf_op jit(solution)/shard_map/pallas_call | solution.py:115
  371.0 6.3 %collective-permute-done.2 = f32[512,1024]{1,0:T(8,128)S(1)} collective-permute-done((f32[512,1024]{1,0:T(8,128)}, f32[512,1024]{1,0:T(8,128)S(1)}, u32[]{:S(2)}, u32[]{:S(2)}) %collective-permute-start.2) | collective-permute-done | bytes 2097184 | tf_op jit(solution)/shard_map/ppermute | solution.py:270
  377.3 2.0 add.42
  379.3 2.7 copy.48
  382.0 10.7 %shard_map.107 = f32[9,4,128]{2,1,0:T(4,128)} custom-call(f32[8,128,4,1024]{3,2,1,0:T(4,128)} %basis_ref.5, f32[128,4,1024]{2,1,0:T(4,128)} %bitcast.54), custom_call_target="tpu_custom_call" | custom-call | tf_op jit(solution)/shard_map/pallas_call | solution.py:197
  393.6 39.8 %psum.7 = f32[45]{0:T(128)S(1)} all-reduce(f32[45]{0:T(128)S(1)} %pad_maximum_fusion.3), channel_id=1, replica_groups=mesh['blk'=16,'cuts'=2] {'blk','cuts'}, use_global_device_ids=true, to_apply=%region_2.3 | all-reduce | flops 45 | bytes 360 | tf_op jit(solution)/shard_map/psum | solution.py:278
  446.0 9.4 %shard_map.108 = f32[128,4,1024]{2,1,0:T(4,128)} custom-call(f32[9]{0:T(128)} %pad_maximum_fusion.4.coef_ref, f32[8,128,4,1024]{3,2,1,0:T(4,128)} %basis_ref.5, f32[128,4,1024]{2,1,0:T(4,128)} %bitcast.55), custom_call_target="tpu_custom_call" | custom-call | tf_op jit(solution)/shard_map/pallas_call | solution.py:222
  (46 shorter events, 11.2 us)
Async XLA Ops:
  7.2 38.0 %copy-start = (f32[8,8,2,2]{1,3,2,0:T(2,128)S(1)}, f32[8,8,2,2]{1,3,2,0:T(2,128)}, u32[]{:S(2)}) copy-start(f32[8,8,2,2]{1,3,2,0:T(2,128)} %param.11) | copy-start | bytes 3076
  7.2 132.8 %all-gather.3.cloned.1.call-start = ((), (), s32[]{:S(2)}) async-start(), calls=%async_computation | async-start | bytes 17825792 | tf_op jit(solution)/shard_map/all_gather | solution.py:262
  9.3 2.0 copy-start.2
  10.7 297.7 %all-gather.5.cloned.1.call-start = ((), (), s32[]{:S(2)}) async-start(), calls=%async_computation.1 | async-start | bytes 35651584 | tf_op jit(solution)/shard_map/all_gather | solution.py:263
  12.6 26.2 %collective-permute-start.1 = (bf16[4,128,1024]{2,1,0:T(8,128)(2,1)S(1)}, bf16[4,128,1024]{2,1,0:T(8,128)(2,1)S(1)}, u32[]{:S(2)}, u32[]{:S(2)}) collective-permute-start(bf16[4,128,1024]{2,1,0:T(8,128)(2,1)S(1)} %bitcast.61), channel_id=1, source_target_pairs={{0,1},{1,0},{2,3},{3,2},{4,5},{5,4},{6,7},{7,6},{8,9},{9,8},{10,11... | collective-permute-start | bytes 3145736 | tf_op jit(solution)/shard_map/ppermute | solution.py:255
  40.4 4.6 copy-start.4
  40.4 4.6 copy-start.5
  43.1 47.1 %collective-permute-start = (bf16[4,128,2048]{2,1,0:T(8,128)(2,1)S(1)}, bf16[4,128,2048]{2,1,0:T(8,128)(2,1)}, u32[]{:S(2)}, u32[]{:S(2)}) collective-permute-start(bf16[4,128,2048]{2,1,0:T(8,128)(2,1)S(1)} %bitcast.57), channel_id=1, source_target_pairs={{0,1},{1,0},{2,3},{3,2},{4,5},{5,4},{6,7},{7,6},{8,9},{9,8},{10,11... | collective-permute-start | bytes 6291464 | tf_op jit(solution)/shard_map/ppermute | solution.py:256
  329.3 48.0 %collective-permute-start.2 = (f32[512,1024]{1,0:T(8,128)}, f32[512,1024]{1,0:T(8,128)S(1)}, u32[]{:S(2)}, u32[]{:S(2)}) collective-permute-start(f32[512,1024]{1,0:T(8,128)} %shard_map.106), channel_id=1, source_target_pairs={{0,1},{1,0},{2,3},{3,2},{4,5},{5,4},{6,7},{7,6},{8,9},{9,8},{10,11... | collective-permute-start | bytes 6291464 | tf_op jit(solution)/shard_map/ppermute | solution.py:270
  331.4 18.7 %copy-start.3 = (s32[64]{0:T(128)S(1)}, s32[64]{0:T(128)}, u32[]{:S(2)}) copy-start(s32[64]{0:T(128)} %constant.58) | copy-start | bytes 772
  446.0 9.4 %copy-start.1 = (f32[8,8,2,2]{1,3,2,0:T(2,128)S(1)}, f32[8,8,2,2]{1,3,2,0:T(2,128)}, u32[]{:S(2)}) copy-start(f32[8,8,2,2]{1,3,2,0:T(2,128)} %param.11) | copy-start | bytes 3076
Sparse Core Ops, SparseCore 0:
  10.8 129.1 all-gather.2
  142.1 166.2 all-gather.4
where the time goes:
time: 464 us; the launch traced here: 463 us
  waiting for transfers between devices  235 us (51%)
  Pallas kernels  124 us (27%)
  blocking collectives  39.8 us (9%)
  between operations  23 us (5%)
  local copies, waits for them, and re-layouts  18.3 us (4%)
  other arithmetic  16 us (3%)
  starting transfers between devices  6.41 us (1%)
    all_gather x1, waiting for transfers between devices, on_device(): right_full = lax.all_gather(right_k, 'blk', axis=1, tiled=True)  124 us
    all_gather x1, waiting for transfers between devices, on_device(): cur_full = lax.all_gather(current, 'blk', axis=1, tiled=True)  45.9 us
    pallas_call x1, Pallas kernels, mixed_left_of(): pl.pallas_call(mix_kernel, grid=(cols // tb,), in_specs=[pl.BlockSpec(mix...  44.8 us
    pallas_call x2, Pallas kernels, image_part(): pl.pallas_call(image_kernel, grid_spec=pltpu.PrefetchScalarGridSpec(num_s...  41.8 us
    psum x1, blocking collectives, on_device(): lax.psum(jnp.concatenate([gram, dots_of(krylov_basis, image)]), ('blk', '...  39.8 us
    ppermute x1, waiting for transfers between devices, on_device(): lax.ppermute(left_t, 'cuts', swap)  36.8 us
    ppermute x1, waiting for transfers between devices, on_device(): lax.ppermute(theirs, 'cuts', swap)  22.8 us
    pallas_call x1, Pallas kernels, gram_of(): pl.pallas_call(gram_kernel, grid=(rows // ta,), in_specs=[pl.BlockSpec((b...  17.4 us
  transfers between devices with their start and end apart: 5, of which 5 were waited for; matrix products, arithmetic and copies ran while one was open for 4% of the time, Pallas kernels for 18%

commit v1 on v0

--- a/solution.py
+++ b/solution.py
@@ -233,19 +233,400 @@
     )(coefs, basis, image)
 
 
-def on_device(
-    cuts, left_env, right_env, left_core, right_core, slot_bond, krylov_basis, beta_prev
+MESH = pl.DeviceIdType.MESH
+
+
+def ring_kernel(
+    vec_ref, left_ref, right_ref, mix_ref, basis_ref,
+    image_ref, gram_ref,
+    vec, left, right, mixed, proj, parts, pair_in, cut_in, gram_buf,
+    own_sem, pre_send, pre_recv, vec_send, vec_recv, right_send, right_recv,
+    pair_send, pair_recv, cut_send, cut_recv, gram_sem,
 ):
-    bond_width = left_core.shape[0]
-    pair_count = left_core.shape[2] * left_core.shape[2]
-    basis_count, row_count, _, col_count = krylov_basis.shape
+    chips, pairs, chip_rows, quarter = vec.shape
+    slots, _, depth = left.shape
+    half_slots, rows, _ = left_ref.shape
+    span = right_ref.shape[3]
+    last = chips - 1
+    polls = 2 * last
+    row_tile, col_tile = proj.shape[2], proj.shape[3]
+    col_tiles = quarter // col_tile
+    mix_units = (chip_rows // row_tile) * col_tiles
+    basis_count = basis_ref.shape[0]
+    gram_rows = gram_buf.shape[2]
+    gram_units = rows // gram_rows
+    half = chips // 2
+
+    blk = lax.axis_index("blk")
+    cut = lax.axis_index("cuts")
+    core = lax.rem(blk, 2)
+    chip = blk // 2
+    side = lax.rem(chip, 2)
+    place = (1 - side) * (chip // 2) + side * (last - chip // 2)
+
+    def chip_at(index):
+        index = lax.rem(index + 2 * chips, chips)
+        far = index // half
+        return (1 - far) * 2 * index + far * (2 * (last - index) + 1)
+
+    after = (2 * chip_at(place + 1) + core, cut)
+    before = (2 * chip_at(place - 1) + core, cut)
+    onward = (after, before)
+    partner = (2 * chip + 1 - core, cut)
+    across = (blk, 1 - cut)
+    corner = (2 * chip + 1 - core, 1 - cut)
+
+    def remote(src, dst, send, recv, device):
+        return pltpu.make_async_remote_copy(
+            src_ref=src, dst_ref=dst, send_sem=send, recv_sem=recv,
+            device_id=device, device_id_type=MESH,
+        )
+
+    def from_place(way, step):
+        return chip_at(place - 1 - step) if way == 0 else chip_at(place + 1 + step)
+
+    def vec_copy(way, step, sub, at):
+        view = vec.at[at, pl.ds(way * (pairs // 2), pairs // 2), pl.ds(sub * rows, rows), :]
+        return remote(
+            view, view, vec_send.at[way, step, sub], vec_recv.at[way, step, sub], onward[way]
+        )
+
+    def right_copy(way, step, sub, at):
+        view = right.at[at, pl.ds(way * rows, rows), pl.ds(sub * span, span)]
+        return remote(
+            view, view, right_send.at[way, step, sub], right_recv.at[way, step, sub], onward[way]
+        )
+
+    def poll(copy_of, index):
+        step, sub = index // 2, lax.rem(index, 2)
+        for way in range(2):
+            at = from_place(way, step)
+            copy_of(way, step, sub, at).wait_recv()
+
+            @pl.when(step < last - 1)
+            def _():
+                copy_of(way, step + 1, sub, at).start()
+
+    def drain(copy_of):
+        @pl.loop(0, polls)
+        def _(index):
+            for way in range(2):
+                copy_of(way, index // 2, lax.rem(index, 2), chip).wait_send()
+
+    mine = pl.ds(core * rows, rows)
+    vec_own = pltpu.make_async_copy(vec_ref.at[core], vec.at[chip, :, mine, :], own_sem.at[0])
+    left_view = left.at[pl.ds(cut * half_slots, half_slots), mine, :]
+    left_other = left.at[pl.ds((1 - cut) * half_slots, half_slots), mine, :]
+    left_own = pltpu.make_async_copy(left_ref, left_view, own_sem.at[1])
+    right_view = right.at[chip, mine, pl.ds(cut * span, span)]
+    right_own = pltpu.make_async_copy(right_ref.at[cut, core], right_view, own_sem.at[2])
+    vec_own.start()
+    left_own.start()
+    right_own.start()
+
+    def gram_copy(unit):
+        slot = lax.rem(unit, 2)
+        return pltpu.make_async_copy(
+            basis_ref.at[:, pl.ds(unit * gram_rows, gram_rows), :, :],
+            gram_buf.at[slot],
+            gram_sem.at[slot],
+        )
+
+    barrier = pltpu.get_barrier_semaphore()
+    friends = (after, before, partner, across, corner)
+    for friend in friends:
+        pl.semaphore_signal(barrier, inc=1, device_id=friend, device_id_type=MESH)
+    pl.semaphore_wait(barrier, len(friends))
+
+    vec_pre = remote(
+        vec_ref.at[1 - core], vec.at[chip, :, mine, :], pre_send.at[0], pre_recv.at[0], partner
+    )
+    vec_pre.start()
+    left_across = remote(left_ref, left_view, pre_send.at[1], pre_recv.at[1], across)
+    left_across.start()
+    right_pre = (
+        remote(right_ref.at[1 - cut, core], right_view, pre_send.at[2], pre_recv.at[2], across),
+        remote(
+            right_ref.at[1 - cut, 1 - core], right_view, pre_send.at[3], pre_recv.at[3], corner
+        ),
+        remote(right_ref.at[cut, 1 - core], right_view, pre_send.at[4], pre_recv.at[4], partner),
+    )
+    for copy in right_pre:
+        copy.start()
+    left_pair = remote(left_ref, left_view, pre_send.at[5], pre_recv.at[5], partner)
+    left_pair.start()
+    gram_copy(0).start()
+    gram_ref[...] = jnp.zeros_like(gram_ref)
+
+    vec_own.wait()
+    vec_pre.wait_recv()
+    for sub in range(2):
+        for way in range(2):
+            vec_copy(way, 0, sub, chip).start()
+
+    def gram_unit(unit):
+        slot = lax.rem(unit, 2)
+        gram_copy(unit).wait()
+
+        @pl.when(unit + 1 < gram_units)
+        def _():
+            gram_copy(unit + 1).start()
+
+        chunk = 4
+
+        @pl.loop(0, gram_rows // chunk)
+        def _(r):
+            for c in range(gram_buf.shape[4] // 128):
+                vecs = [
+                    gram_buf[slot, j, pl.ds(r * chunk, chunk), :, c * 128 : (c + 1) * 128]
+                    for j in range(basis_count)
+                ]
+                i = 0
+                for j in range(basis_count):
+                    for k in range(j, basis_count):
+                        gram_ref[i] += jnp.sum(vecs[j] * vecs[k], axis=0)
+                        i += 1
+
+    @pl.loop(0, polls - 2)
+    def _(index):
+        poll(vec_copy, index)
+
+        @pl.when(index < gram_units)
+        def _():
+            gram_unit(index)
+
+    right_own.wait()
+    for copy in right_pre:
+        copy.wait_recv()
+    for sub in range(2):
+        for way in range(2):
+            right_copy(way, 0, sub, chip).start()
+
+    left_across.wait_recv()
+    left_pass = remote(left_other, left_other, pre_send.at[6], pre_recv.at[6], partner)
+    left_pass.start()
+
+    @pl.loop(polls - 2, polls)
+    def _(index):
+        poll(vec_copy, index)
+
+    left_own.wait()
+    left_pair.wait_recv()
+    left_pass.wait_recv()
+
+    def mix_unit(unit):
+        row0 = pl.multiple_of((unit // col_tiles) * row_tile, row_tile)
+        col0 = pl.multiple_of(lax.rem(unit, col_tiles) * col_tile, col_tile)
+
+        @pl.loop(0, pairs)
+        def _(q):
+            proj[q] = jnp.dot(
+                left[:, pl.ds(row0, row_tile), :].reshape(slots * row_tile, depth),
+                vec[:, q, :, pl.ds(col0, col_tile)].reshape(depth, col_tile),
+                preferred_element_type=jnp.float32,
+            ).reshape(slots, row_tile, col_tile)
+
+        owner = row0 // rows
+        base = owner * (pairs * rows) + row0 - owner * rows
+
+        @pl.loop(0, row_tile // 16)
+        def _(g):
+            lines = []
+            for h in range(2):
+                at = pl.ds(pl.multiple_of(g * 16 + h * 8, 8), 8)
+                stacked = jnp.concatenate(
+                    [proj[q, k, at, :] for k in range(slots) for q in range(pairs)], axis=0
+                )
+                lines.append(
+                    jnp.dot(
+                        mix_ref[...],
+                        stacked,
+                        precision=lax.Precision.HIGHEST,
+                        preferred_element_type=jnp.float32,
+                    )
+                )
+            for y in range(slots):
+                cols = pl.ds(pl.multiple_of(y * quarter + col0, col_tile), col_tile)
+                for p in range(pairs):
+                    i = (y * pairs + p) * 8
+                    at = pl.ds(pl.multiple_of(base + p * rows + g * 16, 16), 16)
+                    mixed[at, cols] = jnp.concatenate(
+                        [m[i : i + 8] for m in lines], axis=0
+                    ).astype(mixed.dtype)
+
+    lot = pairs * rows
+
+    def pair_copy(unit):
+        return remote(
+            parts.at[chips + lax.rem(unit, 2)], pair_in.at[unit],
+            pair_send.at[unit], pair_recv.at[unit], partner,
+        )
+
+    def block_of(unit, way):
+        return chip_at(place - unit) if way == 0 else chip_at(place + unit)
+
+    def home_of(unit, way):
+        at = block_of(unit, way)
+        return at // half, lax.rem(at, half) * 2 + way
+
+    def cut_copy(unit, way):
+        _, piece = home_of(unit, way)
+        return remote(
+            parts.at[unit, way], cut_in.at[piece],
+            cut_send.at[unit, way], cut_recv.at[piece], across,
+        )
+
+    def image_unit(unit):
+        @pl.when(unit >= 2)
+        def _():
+            pair_copy(unit - 2).wait_send()
+
+        @pl.loop(0, 2)
+        def _(k):
+            owner = lax.rem(core + 1 + k, 2)
+            to = (1 - k) * (chips + lax.rem(unit, 2)) + k * unit
+            lines = jnp.concatenate(
+                [right[block_of(unit, way), way * rows : (way + 1) * rows, :] for way in range(2)],
+                axis=0,
+            )
+            out = lax.dot_general(
+                mixed[pl.ds(pl.multiple_of(owner * lot, lot), lot), :],
+                lines,
+                (((1,), (1,)), ((), ())),
+                preferred_element_type=jnp.float32,
+            )
+            for way in range(2):
+                parts[to, way] = out[:, way * rows : (way + 1) * rows].reshape(pairs, rows, rows)
+
+        pair_copy(unit).start()
+
+    def join_unit(unit):
+        pair_copy(unit).wait_recv()
+        for way in range(2):
+            parts[unit, way] += pair_in[unit, way]
+            home, _ = home_of(unit, way)
+
+            @pl.when(home != cut)
+            def _():
+                cut_copy(unit, way).start()
+
+    @pl.loop(0, mix_units)
+    def _(index):
+        poll(right_copy, index)
+        mix_unit(index)
+
+    def ready(index):
+        return jnp.minimum(2 * (index - mix_units + 1), (index + 1) // 2 + 1)
+
+    @pl.loop(mix_units, polls)
+    def _(index):
+        poll(right_copy, index)
+
+        @pl.loop(ready(index - 1), ready(index))
+        def _(unit):
+            image_unit(unit)
+
+            @pl.when(unit > 0)
+            def _():
+                join_unit(unit - 1)
+
+    join_unit(last)
+
+    @pl.loop(0, chips)
+    def _(unit):
+        for way in range(2):
+            home, piece = home_of(unit, way)
+            copy = cut_copy(unit, way)
+
+            @pl.when(home == cut)
+            def _():
+                copy.wait_recv()
+                cols = pl.ds(pl.multiple_of(piece * rows, rows), rows)
+                image_ref[:, :, cols] = parts[unit, way] + cut_in[piece]
+
+            @pl.when(home != cut)
+            def _():
+                copy.wait_send()
+
+    drain(vec_copy)
+    drain(right_copy)
+    for unit in (chips - 2, chips - 1):
+        pair_copy(unit).wait_send()
+    vec_pre.wait_send()
+    left_across.wait_send()
+    for copy in right_pre:
+        copy.wait_send()
+    left_pair.wait_send()
+    left_pass.wait_send()
+
+
+def ring_image(table, left_env, right_env, current, basis):
+    rows, half_slots, depth = left_env.shape
+    pairs, cols = current.shape[1], current.shape[2]
+    slots, chips, quarter = 2 * half_slots, depth // (2 * rows), cols // 2
+    basis_count = basis.shape[0]
+    count = basis_count * (basis_count + 1) // 2
+    square = table.transpose(1, 2, 0, 3).reshape(slots * pairs, slots * pairs)
+    mix = jnp.kron(square, jnp.eye(8, dtype=jnp.float32))
+    vec = current.reshape(rows, pairs, 2, quarter).transpose(2, 1, 0, 3)
+    left = left_env.transpose(1, 0, 2)
+    right = right_env.reshape(rows, half_slots, 2, 2, quarter).transpose(2, 3, 0, 1, 4)
+    right = right.reshape(2, 2, rows, half_slots * quarter)
+    bf16, f32 = jnp.bfloat16, jnp.float32
+    sem = pltpu.SemaphoreType.DMA
+    steps = chips - 1
+    hbm = pl.BlockSpec(memory_space=pltpu.HBM)
+    vmem = pl.BlockSpec(memory_space=pltpu.VMEM)
+    return pl.pallas_call(
+        ring_kernel,
+        name="ring",
+        in_specs=[hbm, hbm, hbm, vmem, hbm],
+        out_specs=[vmem, vmem],
+        out_shape=[
+            jax.ShapeDtypeStruct((pairs, rows, cols), f32),
+            jax.ShapeDtypeStruct((count, pairs, 128), f32),
+        ],
+        scratch_shapes=[
+            pltpu.VMEM((chips, pairs, 2 * rows, quarter), bf16),
+            pltpu.VMEM((slots, 2 * rows, depth), bf16),
+            pltpu.VMEM((chips, 2 * rows, slots * quarter), bf16),
+            pltpu.VMEM((2 * pairs * rows, slots * quarter), bf16),
+            pltpu.VMEM((pairs, slots, rows // 2, quarter // 2), f32),
+            pltpu.VMEM((chips + 2, 2, pairs, rows, rows), f32),
+            pltpu.VMEM((chips, 2, pairs, rows, rows), f32),
+            pltpu.VMEM((chips, pairs, rows, rows), f32),
+            pltpu.VMEM((2, basis_count, rows // 8, pairs, cols), f32),
+            sem((3,)),
+            sem((7,)),
+            sem((7,)),
+            sem((2, steps, 2)),
+            sem((2, steps, 2)),
+            sem((2, steps, 2)),
+            sem((2, steps, 2)),
+            sem((chips,)),
+            sem((chips,)),
+            sem((chips, 2)),
+            sem((chips,)),
+            sem((2,)),
+        ],
+        compiler_params=pltpu.CompilerParams(
+            vmem_limit_bytes=63 * 1024 * 1024, collective_id=1, has_side_effects=True
+        ),
+    )(vec, left, right, mix, basis)
+
+
+def ring_fits(blocks, rows, depth):
+    return blocks == 16 and rows * blocks == depth and rows % 128 == 0
+
+
+def gathered_image(cuts, table, left_env, right_env, current):
+    row_count, pair_count, col_count = current.shape
+    bond_width = table.shape[0]
     full_width = left_env.shape[2]
-    entries = float(full_width * pair_count * full_width)
-    table = build_table(left_core, right_core, slot_bond)
     me = lax.axis_index("cuts")
     swap = [(0, 1), (1, 0)]
 
-    current = krylov_basis[basis_count - 1].astype(jnp.bfloat16).transpose(1, 0, 2)
+    current = current.transpose(1, 0, 2)
     left_t = left_env.transpose(1, 0, 2)
     right_t = right_env.transpose(1, 0, 2)
     if cuts == 2:
@@ -261,7 +642,6 @@
         right_k = lax.all_to_all(right_t, "cuts", split_axis=2, concat_axis=0, tiled=True)
     cur_full = lax.all_gather(current, "blk", axis=1, tiled=True)
     right_full = lax.all_gather(right_k, "blk", axis=1, tiled=True)
-    gram = gram_of(krylov_basis)
 
     mixed = mixed_left_of(table, left_k, cur_full)
     mixed = mixed.reshape(bond_width, pair_count * row_count, col_count)
@@ -273,7 +653,25 @@
     else:
         image = image_part(mixed, right_full, jnp.int32(0), full_width)
         image = lax.psum_scatter(image, "cuts", scatter_dimension=1, tiled=True)
-    image = image.reshape(pair_count, row_count, col_count).transpose(1, 0, 2)
+    return image.reshape(pair_count, row_count, col_count).transpose(1, 0, 2)
+
+
+def on_device(
+    blocks, cuts, left_env, right_env, left_core, right_core, slot_bond, krylov_basis, beta_prev
+):
+    pair_count = left_core.shape[2] * left_core.shape[2]
+    basis_count, row_count, _, _ = krylov_basis.shape
+    full_width = left_env.shape[2]
+    entries = float(full_width * pair_count * full_width)
+    table = build_table(left_core, right_core, slot_bond)
+    current = krylov_basis[basis_count - 1].astype(jnp.bfloat16)
+    if cuts == 2 and ring_fits(blocks, row_count, full_width):
+        image, gram = ring_image(table, left_env, right_env, current, krylov_basis)
+        image = image.transpose(1, 0, 2)
+        gram = jnp.sum(gram, axis=(1, 2))
+    else:
+        image = gathered_image(cuts, table, left_env, right_env, current)
+        gram = gram_of(krylov_basis)
 
     sums = lax.psum(jnp.concatenate([gram, dots_of(krylov_basis, image)]), ("blk", "cuts"))
     sums = sums / entries
@@ -328,7 +726,7 @@
     )
     out_specs = (P("blk", None, "cuts"), P(), P())
     return jax.shard_map(
-        functools.partial(on_device, mesh.shape["cuts"]),
+        functools.partial(on_device, mesh.shape["blk"], mesh.shape["cuts"]),
         mesh=mesh,
         in_specs=in_specs,
         out_specs=out_specs,

time: 464 us -> 374 us (0.81)
  waiting for transfers between devices: 235 us -> 0 us
  Pallas kernels: 124 us -> 290 us
  between operations: 23 us -> 9.8 us
  local copies, waits for them, and re-layouts: 18.3 us -> 28.5 us
  other arithmetic: 16 us -> 7.36 us
  starting transfers between devices: 6.41 us -> 0 us
    all_gather x2 -> x0, waiting for transfers between devices: 169 us -> none  [the longest x1 124 us: on_device(): right_full = lax.all_gather(right_k, 'blk', axis=1, tiled=True)]
    pallas_call x4 -> x1, Pallas kernels: 104 us -> 270 us  [ring_image(): pl.pallas_call(ring_kernel, name='ring', in_specs=[hbm, hbm, hbm, vmem, h...]
    ppermute x3 -> x0, waiting for transfers between devices: 65.9 us -> none  [the longest x1 36.8 us: on_device(): lax.ppermute(left_t, 'cuts', swap)]
    reshape x1 -> x3, local copies, waits for them, and re-layouts: 2.7 us -> 9.59 us  [the longest x2 6.78 us: ring_image(): right_env.reshape(rows, half_slots, 2, 2, quarter).transpose(2, 3, 0, 1, 4)]
    ppermute x3 -> x0, starting transfers between devices: 6.33 us -> none  [the longest x1 3.06 us: on_device(): lax.ppermute(theirs, 'cuts', swap)]
    concatenate x3 -> x0, other arithmetic: 5.52 us -> none  [the longest x1 3.92 us: on_device(): jnp.concatenate([left_t, lax.ppermute(left_t, 'cuts', swap)], axis=0)]
  transfers between devices with their start and end apart: 5 -> 0, of which waited for: 5 -> 0; matrix products, arithmetic and copies ran while one was open for 4% -> 0% of each run, Pallas kernels for 18% -> 0%
where the time goes in v1:
time: 374 us; the launch traced here: 373 us
  Pallas kernels  290 us (78%)
  blocking collectives  37.7 us (10%)
  local copies, waits for them, and re-layouts  28.5 us (8%)
  between operations  9.8 us (3%)
  other arithmetic  7.36 us (2%)
    pallas_call x1, Pallas kernels, ring_image(): pl.pallas_call(ring_kernel, name='ring', in_specs=[hbm, hbm, hbm, vmem, h...  270 us
    psum x1, blocking collectives, on_device(): lax.psum(jnp.concatenate([gram, dots_of(krylov_basis, image)]), ('blk', '...  37.7 us
    pallas_call x1, Pallas kernels, dots_of(): pl.pallas_call(dots_kernel, grid=(rows // ta,), in_specs=[pl.BlockSpec((b...  10.8 us
    pallas_call x1, Pallas kernels, final_of(): pl.pallas_call(final_kernel, grid=(rows // ta,), in_specs=[pl.BlockSpec(m...  9.42 us

profile of v1, /device:TPU:0, one launch (start us, length us, event | category | flops | bytes accessed | tf_op | source)
XLA Modules:
  0.0 373.5 jit_solution(10285814088149807779)
XLA Ops:
  0.6 4.4 %reshape.50 = bf16[128,4,2,2,512]{4,3,2,1,0:T(2,128)(2,1)} reshape(bf16[128,4,2048]{2,1,0:T(4,128)(2,1)} %param.9) | data formatting | bytes 4194304 | tf_op jit(solution)/shard_map/reshape | solution.py:573
  5.0 2.4 copy.38
  7.5 2.8 reshape.51.right_ref
  11.1 2.5 broadcast_multiply_fusion
  13.6 4.7 %mul.113.mix_ref = f32[256,256]{1,0:T(8,128)} reshape(f32[32,8,32,8]{3,2,1,0:T(8,128)} %broadcast_multiply_fusion) | data formatting | bytes 524288 | tf_op jit(solution)/shard_map/jit(kron)/mul | solution.py:570
  18.3 2.1 slice.46
  20.3 1.0 copy.29
  21.3 1.3 copy.16
  22.7 0.6 copy-done.1
  23.3 2.5 copy.39
  25.8 269.5 %ring.1 = (f32[4,128,1024]{2,1,0:T(8,128)}, f32[36,4,128]{2,1,0:T(4,128)}) custom-call(bf16[2,4,128,512]{3,2,1,0:T(8,128)(2,1)} %bitcast.44, bf16[4,128,2048]{2,1,0:T(8,128)(2,1)} %bitcast.43, bf16[2,2,128,2048]{3,2,1,0:T(8,128)(2,1)} %reshape.51.right_ref, f32[256,256]{1,0:T(8,128)} %mul.113.mix_ref, f32[8,128,4,1024]{3,2,1,0:T(4,128)} %basis_ref.5), custom_call_target="tpu_custom_call" | custom-call | tf_op jit(solution)/shard_map/ring/pallas_call | solution.py:580
  295.3 4.2 %copy.37 = f32[4,128,1024]{2,0,1:T(4,128)} copy(f32[4,128,1024]{2,1,0:T(8,128)} %get-tuple-element.6) | data formatting | bytes 4194304 | tf_op jit(solution)/shard_map/ring/pallas_call | solution.py:580
  299.6 10.8 %shard_map.103 = f32[9,4,128]{2,1,0:T(4,128)} custom-call(f32[8,128,4,1024]{3,2,1,0:T(4,128)} %basis_ref.5, f32[128,4,1024]{2,1,0:T(4,128)} %bitcast.40), custom_call_target="tpu_custom_call" | custom-call | tf_op jit(solution)/shard_map/pallas_call | solution.py:197
  310.3 0.9 reduce_sum.37
  311.6 37.7 %psum.7 = f32[45]{0:T(128)S(1)} all-reduce(f32[45]{0:T(128)S(1)} %pad_maximum_fusion), channel_id=1, replica_groups=mesh['blk'=16,'cuts'=2] {'blk','cuts'}, use_global_device_ids=true, to_apply=%region_2.3 | all-reduce | flops 45 | bytes 360 | tf_op jit(solution)/shard_map/psum | solution.py:676
  349.3 0.6 fusion.9
  354.5 0.8 gather_fusion
  355.3 0.7 fusion.8
  358.0 0.9 multiply_reduce_fusion.2
  358.9 0.7 fusion.7
  359.6 0.6 multiply_reduce_fusion.3
  360.9 0.7 multiply_reduce_fusion
  362.3 0.7 pad_maximum_fusion.1.coef_ref
  362.9 9.4 %shard_map.104 = f32[128,4,1024]{2,1,0:T(4,128)} custom-call(f32[9]{0:T(128)} %pad_maximum_fusion.1.coef_ref, f32[8,128,4,1024]{3,2,1,0:T(4,128)} %basis_ref.5, f32[128,4,1024]{2,1,0:T(4,128)} %bitcast.41), custom_call_target="tpu_custom_call" | custom-call | tf_op jit(solution)/shard_map/pallas_call | solution.py:222
  (22 shorter events, 1.3 us)
Async XLA Ops:
  0.6 9.8 %copy-start = (f32[8,8,2,2]{1,3,2,0:T(2,128)S(1)}, f32[8,8,2,2]{1,3,2,0:T(2,128)}, u32[]{:S(2)}) copy-start(f32[8,8,2,2]{1,3,2,0:T(2,128)} %param.11) | copy-start | bytes 3076
  7.4 2.8 copy-start.4
  7.4 2.8 copy-start.5
  21.3 2.0 copy-start.1
  299.6 11.6 %copy-start.2 = (f32[36,4,128]{2,1,0:T(4,128)S(1)}, f32[36,4,128]{2,1,0:T(4,128)}, u32[]{:S(2)}) copy-start(f32[36,4,128]{2,1,0:T(4,128)} %get-tuple-element.5) | copy-start | bytes 221188
  299.6 54.9 %copy-start.3 = (s32[64]{0:T(128)S(1)}, s32[64]{0:T(128)}, u32[]{:S(2)}) copy-start(s32[64]{0:T(128)} %constant.26) | copy-start | bytes 772

commit v2 on v1

--- a/solution.py
+++ b/solution.py
@@ -542,7 +542,9 @@
             def _():
                 copy.wait_recv()
                 cols = pl.ds(pl.multiple_of(piece * rows, rows), rows)
-                image_ref[:, :, cols] = parts[unit, way] + cut_in[piece]
+                whole = parts[unit, way] + cut_in[piece]
+                for p in range(pairs):
+                    image_ref[:, p, cols] = whole[p]
 
             @pl.when(home != cut)
             def _():
@@ -583,7 +585,7 @@
         in_specs=[hbm, hbm, hbm, vmem, hbm],
         out_specs=[vmem, vmem],
         out_shape=[
-            jax.ShapeDtypeStruct((pairs, rows, cols), f32),
+            jax.ShapeDtypeStruct((rows, pairs, cols), f32),
             jax.ShapeDtypeStruct((count, pairs, 128), f32),
         ],
         scratch_shapes=[
@@ -615,6 +617,173 @@
     )(vec, left, right, mix, basis)
 
 
+def finish_kernel(
+    blocks, cuts, entries,
+    beta_ref, gram_ref, image_ref, basis_ref,
+    next_ref, values_ref,
+    basis, tile, inbox, load_sem, send_sem, recv_sem,
+):
+    basis_count, rows, pairs, cols = basis.shape
+    chunks = load_sem.shape[0]
+    chunk = rows // chunks
+    lanes = cols // 128
+    devices = blocks * cuts
+    me = lax.axis_index("blk") * cuts + lax.axis_index("cuts")
+
+    def load(unit):
+        at = pl.ds(unit * chunk, chunk)
+        return pltpu.make_async_copy(
+            basis_ref.at[:, at, :, :], basis.at[:, at, :, :], load_sem.at[unit]
+        )
+
+    for unit in range(chunks):
+        load(unit).start()
+
+    def place(offset):
+        device = lax.rem(me + offset, devices)
+        return (device // cuts, lax.rem(device, cuts))
+
+    barrier = pltpu.get_barrier_semaphore()
+    for offset in range(1, devices):
+        pl.semaphore_signal(barrier, inc=1, device_id=place(offset), device_id_type=MESH)
+
+    row = lax.broadcasted_iota(jnp.int32, tile.shape, 0)
+    lane = lax.broadcasted_iota(jnp.int32, tile.shape, 1)
+
+    def total_of(x):
+        return jnp.sum(jnp.sum(x, axis=0, keepdims=True), axis=1, keepdims=True)
+
+    found = jnp.zeros(tile.shape, jnp.float32)
+    i = 0
+    for j in range(basis_count):
+        for k in range(j, basis_count):
+            here = ((row == j) & (lane == k)) | ((row == k) & (lane == j))
+            found = jnp.where(here, total_of(gram_ref[i]), found)
+            i += 1
+    tile[...] = found
+
+    def dots(unit, sums):
+        load(unit).wait()
+        for c in range(lanes):
+            at = slice(c * 128, (c + 1) * 128)
+            for step in range(chunk // 8):
+                r = pl.ds(unit * chunk + step * 8, 8)
+                image = image_ref[r, :, at]
+                sums = tuple(
+                    sums[j] + jnp.sum(basis[j, r, :, at] * image, axis=0)
+                    for j in range(basis_count)
+                ) + (sums[basis_count] + jnp.sum(image * image, axis=0),)
+        return sums
+
+    zero = jnp.zeros((pairs, 128), jnp.float32)
+    sums = lax.fori_loop(0, chunks, dots, (zero,) * (basis_count + 1))
+    found = tile[...]
+    for j in range(basis_count + 1):
+        here = ((row == j) & (lane == basis_count)) | ((row == basis_count) & (lane == j))
+        found = jnp.where(here, total_of(sums[j]), found)
+    tile[...] = found
+    inbox[me] = found
+
+    pl.semaphore_wait(barrier, devices - 1)
+
+    def send(offset):
+        return pltpu.make_async_remote_copy(
+            src_ref=tile, dst_ref=inbox.at[me],
+            send_sem=send_sem.at[offset], recv_sem=recv_sem.at[offset],
+            device_id=place(offset), device_id_type=MESH,
+        )
+
+    for offset in range(1, devices):
+        send(offset).start()
+    for offset in range(1, devices):
+        send(offset).wait_recv()
+
+    sums = inbox[0]
+    for d in range(1, devices):
+        sums = sums + inbox[d]
+    sums = sums / entries
+    n, last, prior = basis_count, basis_count - 1, basis_count - 2
+    gram = sums[0:n, 0:n]
+    down, along = sums[0:n, n : n + 1], sums[n : n + 1, 0:n]
+    square = sums[n : n + 1, n : n + 1]
+    alpha = down[last : last + 1]
+    beta = jnp.full((1, 1), beta_ref[0], jnp.float32)
+    ortho = down - alpha * gram[:, last : last + 1] - beta * gram[:, prior : prior + 1]
+    ortho_row = along - alpha * gram[last : last + 1, :] - beta * gram[prior : prior + 1, :]
+    first = (
+        square
+        - 2.0 * alpha * alpha
+        - 2.0 * beta * down[prior : prior + 1]
+        + alpha * alpha * gram[last : last + 1, last : last + 1]
+        + 2.0 * alpha * beta * gram[last : last + 1, prior : prior + 1]
+        + beta * beta * gram[prior : prior + 1, prior : prior + 1]
+    )
+    bent = jnp.sum(ortho * gram, axis=0, keepdims=True) * ortho_row
+    mean = (
+        first
+        - 2.0 * jnp.sum(ortho * ortho, axis=0, keepdims=True)
+        + jnp.sum(bent, axis=1, keepdims=True)
+    )
+    beta_new = jnp.sqrt(mean + 1e-06)
+    values_ref[...] = jnp.where(
+        (row == 0) & (lane == 0), alpha, jnp.where((row == 0) & (lane == 1), beta_new, 0.0)
+    )
+    index = lax.broadcasted_iota(jnp.int32, ortho.shape, 0)
+    coefs = (
+        ortho + jnp.where(index == last, alpha, 0.0) + jnp.where(index == prior, beta, 0.0)
+    )
+    spread = [jnp.broadcast_to(coefs[j : j + 1], (pairs, 128)) for j in range(n)]
+    scale = jnp.broadcast_to(1.0 / beta_new, (pairs, 128))
+
+    @pl.loop(0, rows // 8)
+    def _(step):
+        r = pl.ds(step * 8, 8)
+        for c in range(lanes):
+            at = slice(c * 128, (c + 1) * 128)
+            value = image_ref[r, :, at]
+            for j in range(n):
+                value = value - spread[j][None] * basis[j, r, :, at]
+            next_ref[r, :, at] = value * scale[None]
+
+    for offset in range(1, devices):
+        send(offset).wait_send()
+
+
+def finish(blocks, cuts, entries, beta_prev, gram, image, basis):
+    basis_count, rows, pairs, cols = basis.shape
+    tile = (16, 128)
+    devices = blocks * cuts
+    sem = pltpu.SemaphoreType.DMA
+    vmem = pl.BlockSpec(memory_space=pltpu.VMEM)
+    next_vector, values = pl.pallas_call(
+        functools.partial(finish_kernel, blocks, cuts, entries),
+        name="finish",
+        in_specs=[
+            pl.BlockSpec(memory_space=pltpu.SMEM),
+            vmem,
+            vmem,
+            pl.BlockSpec(memory_space=pltpu.HBM),
+        ],
+        out_specs=[vmem, vmem],
+        out_shape=[
+            jax.ShapeDtypeStruct((rows, pairs, cols), jnp.float32),
+            jax.ShapeDtypeStruct(tile, jnp.float32),
+        ],
+        scratch_shapes=[
+            pltpu.VMEM(basis.shape, jnp.float32),
+            pltpu.VMEM(tile, jnp.float32),
+            pltpu.VMEM((devices,) + tile, jnp.float32),
+            sem((rows // 16,)),
+            sem((devices,)),
+            sem((devices,)),
+        ],
+        compiler_params=pltpu.CompilerParams(
+            vmem_limit_bytes=40 * 1024 * 1024, collective_id=2, has_side_effects=True
+        ),
+    )(beta_prev.reshape(1), gram, image, basis)
+    return next_vector, values[0, 0:1], values[0, 1:2]
+
+
 def ring_fits(blocks, rows, depth):
     return blocks == 16 and rows * blocks == depth and rows % 128 == 0
 
@@ -667,11 +836,9 @@
     current = krylov_basis[basis_count - 1].astype(jnp.bfloat16)
     if cuts == 2 and ring_fits(blocks, row_count, full_width):
         image, gram = ring_image(table, left_env, right_env, current, krylov_basis)
-        image = image.transpose(1, 0, 2)
-        gram = jnp.sum(gram, axis=(1, 2))
-    else:
-        image = gathered_image(cuts, table, left_env, right_env, current)
-        gram = gram_of(krylov_basis)
+        return finish(blocks, cuts, entries, beta_prev, gram, image, krylov_basis)
+    image = gathered_image(cuts, table, left_env, right_env, current)
+    gram = gram_of(krylov_basis)
 
     sums = lax.psum(jnp.concatenate([gram, dots_of(krylov_basis, image)]), ("blk", "cuts"))
     sums = sums / entries

time: 374 us -> 319 us (0.85)
  blocking collectives: 37.7 us -> 0 us
  between operations: 9.8 us -> 1.39 us
  other arithmetic: 7.36 us -> 2.54 us
    psum x1 -> x0, blocking collectives: 37.7 us -> none  [on_device(): lax.psum(jnp.concatenate([gram, dots_of(krylov_basis, image)]), ('blk', '...]
    pallas_call x1 -> x0, local copies, waits for them, and re-layouts: 4.24 us -> none  [ring_image(): pl.pallas_call(ring_kernel, name='ring', in_specs=[hbm, hbm, hbm, vmem, h...]
    unnamed x14 -> x15, local copies, waits for them, and re-layouts: 4.12 us -> 7.91 us
    pallas_call x2 -> x1, Pallas kernels: 20.2 us -> 18 us  [finish(): pl.pallas_call(functools.partial(finish_kernel, blocks, cuts, entries), n...]
where the time goes in v2:
time: 319 us; the launch traced here: 318 us
  Pallas kernels  288 us (90%)
  local copies, waits for them, and re-layouts  26.5 us (8%)
    pallas_call x1, Pallas kernels, ring_image(): pl.pallas_call(ring_kernel, name='ring', in_specs=[hbm, hbm, hbm, vmem, h...  270 us
    pallas_call x1, Pallas kernels, finish(): pl.pallas_call(functools.partial(finish_kernel, blocks, cuts, entries), n...  18 us
    unnamed x15, local copies, waits for them, and re-layouts  7.91 us
    reshape x2, local copies, waits for them, and re-layouts, ring_image(): right_env.reshape(rows, half_slots, 2, 2, quarter).transpose(2, 3, 0, 1, 4)  6.78 us

profile of v2, /device:TPU:0, one launch (start us, length us, event | category | flops | bytes accessed | tf_op | source)
XLA Modules:
  0.0 318.4 jit_solution(8400323553798027621)
XLA Ops:
  0.6 0.0 copy-start
  0.6 4.4 %reshape.39 = bf16[128,4,2,2,512]{4,3,2,1,0:T(2,128)(2,1)} reshape(bf16[128,4,2048]{2,1,0:T(4,128)(2,1)} %param.8) | data formatting | bytes 4194304 | tf_op jit(solution)/shard_map/reshape | solution.py:575
  5.0 2.4 copy.33
  7.4 0.0 copy-start.4
  7.4 0.0 copy-start.5
  7.5 2.8 reshape.40.right_ref
  10.2 0.2 convolution_bitcast_fusion.1
  10.4 0.2 convolution_bitcast_fusion
  10.6 0.3 copy.19
  10.9 0.1 mul.26
  11.0 2.5 broadcast_multiply_fusion
  13.6 4.7 %mul.30.mix_ref = f32[256,256]{1,0:T(8,128)} reshape(f32[32,8,32,8]{3,2,1,0:T(8,128)} %broadcast_multiply_fusion) | data formatting | bytes 524288 | tf_op jit(solution)/shard_map/jit(kron)/mul | solution.py:572
  18.2 2.1 slice.13
  20.3 1.0 copy.26
  21.3 0.0 copy-start.3
  21.3 1.3 copy.14
  22.6 0.6 copy-done.3
  23.3 2.5 copy.34
  25.7 269.7 %ring.1 = (f32[128,4,1024]{2,1,0:T(4,128)}, f32[36,4,128]{2,1,0:T(4,128)}) custom-call(bf16[2,4,128,512]{3,2,1,0:T(8,128)(2,1)} %bitcast.35, bf16[4,128,2048]{2,1,0:T(8,128)(2,1)} %bitcast.34, bf16[2,2,128,2048]{3,2,1,0:T(8,128)(2,1)} %reshape.40.right_ref, f32[256,256]{1,0:T(8,128)} %mul.30.mix_ref, f32[8,128,4,1024]{3,2,1,0:T(4,128)} %basis_ref.3), custom_call_target="tpu_custom_call" | custom-call | tf_op jit(solution)/shard_map/ring/pallas_call | solution.py:582
  296.1 1.6 copy-done.1
  297.7 0.9 copy-done.2
  298.5 18.0 %finish.1 = (f32[128,4,1024]{2,1,0:T(4,128)S(1)}, f32[16,128]{1,0:T(8,128)S(1)}) custom-call(f32[1]{0:T(128)} %bitcast.31.beta_ref, f32[36,4,128]{2,1,0:T(4,128)S(1)} %copy-done.2, f32[128,4,1024]{2,1,0:T(4,128)S(1)} %copy-done.1, f32[8,128,4,1024]{3,2,1,0:T(4,128)} %basis_ref.3), custom_call_target="tpu_custom_call" | custom-call | tf_op jit(solution)/shard_map/finish/pallas_call | solution.py:758
  316.5 0.6 fusion.6
  317.1 1.3 copy.37
  (7 shorter events, 0.0 us)
Async XLA Ops:
  0.6 9.8 %copy-start = (f32[8,8,2,2]{1,3,2,0:T(2,128)S(1)}, f32[8,8,2,2]{1,3,2,0:T(2,128)}, u32[]{:S(2)}) copy-start(f32[8,8,2,2]{1,3,2,0:T(2,128)} %param.10) | copy-start | bytes 3076
  7.4 2.8 copy-start.4
  7.4 2.8 copy-start.5
  21.3 2.0 copy-start.3
  296.1 1.6 copy-start.1
  297.7 0.9 copy-start.2

commit v3 on v2

--- a/solution.py
+++ b/solution.py
@@ -237,16 +237,16 @@
 
 
 def ring_kernel(
-    vec_ref, left_ref, right_ref, mix_ref, basis_ref,
+    vec_ref, left_ref, right_ref, square_ref, basis_ref,
     image_ref, gram_ref,
-    vec, left, right, mixed, proj, parts, pair_in, cut_in, gram_buf,
+    vec, left, right, mixed, mix_ref, proj, parts, pair_in, cut_in, gram_buf,
     own_sem, pre_send, pre_recv, vec_send, vec_recv, right_send, right_recv,
     pair_send, pair_recv, cut_send, cut_recv, gram_sem,
 ):
     chips, pairs, chip_rows, quarter = vec.shape
     slots, _, depth = left.shape
     half_slots, rows, _ = left_ref.shape
-    span = right_ref.shape[3]
+    span = half_slots * quarter
     last = chips - 1
     polls = 2 * last
     row_tile, col_tile = proj.shape[2], proj.shape[3]
@@ -298,7 +298,7 @@
         )
 
     def poll(copy_of, index):
-        step, sub = index // 2, lax.rem(index, 2)
+        step, sub = index // 2, lax.rem(index + core, 2)
         for way in range(2):
             at = from_place(way, step)
             copy_of(way, step, sub, at).wait_recv()
@@ -314,15 +314,28 @@
                 copy_of(way, index // 2, lax.rem(index, 2), chip).wait_send()
 
     mine = pl.ds(core * rows, rows)
-    vec_own = pltpu.make_async_copy(vec_ref.at[core], vec.at[chip, :, mine, :], own_sem.at[0])
+    vec_own = pltpu.make_async_copy(vec_ref.at[:, :, pl.ds(core * quarter, quarter)], vec.at[chip, :, mine, :], own_sem.at[0])
     left_view = left.at[pl.ds(cut * half_slots, half_slots), mine, :]
     left_other = left.at[pl.ds((1 - cut) * half_slots, half_slots), mine, :]
     left_own = pltpu.make_async_copy(left_ref, left_view, own_sem.at[1])
-    right_view = right.at[chip, mine, pl.ds(cut * span, span)]
-    right_own = pltpu.make_async_copy(right_ref.at[cut, core], right_view, own_sem.at[2])
+
+    def slot_view(slot):
+        return right.at[chip, mine, pl.ds(cut * span + slot * quarter, quarter)]
+
+    def slot_part(slot, to_cut, to_core):
+        return right_ref.at[slot, :, pl.ds((2 * to_cut + to_core) * quarter, quarter)]
+
+    def vec_part(to_core):
+        return vec_ref.at[:, :, pl.ds(to_core * quarter, quarter)]
+
+    right_own = [
+        pltpu.make_async_copy(slot_part(slot, cut, core), slot_view(slot), own_sem.at[2 + slot])
+        for slot in range(half_slots)
+    ]
     vec_own.start()
     left_own.start()
-    right_own.start()
+    for copy in right_own:
+        copy.start()
 
     def gram_copy(unit):
         slot = lax.rem(unit, 2)
@@ -339,30 +352,49 @@
     pl.semaphore_wait(barrier, len(friends))
 
     vec_pre = remote(
-        vec_ref.at[1 - core], vec.at[chip, :, mine, :], pre_send.at[0], pre_recv.at[0], partner
+        vec_part(1 - core), vec.at[chip, :, mine, :], pre_send.at[0], pre_recv.at[0], partner
     )
     vec_pre.start()
+    right_pre = []
+    for way, (to_cut, to_core, device) in enumerate((
+        (1 - cut, core, across), (1 - cut, 1 - core, corner), (cut, 1 - core, partner)
+    )):
+        for slot in range(half_slots):
+            index = 4 + way * half_slots + slot
+            right_pre.append(remote(
+                slot_part(slot, to_cut, to_core), slot_view(slot),
+                pre_send.at[index], pre_recv.at[index], device,
+            ))
+    for copy in right_pre:
+        copy.start()
     left_across = remote(left_ref, left_view, pre_send.at[1], pre_recv.at[1], across)
     left_across.start()
-    right_pre = (
-        remote(right_ref.at[1 - cut, core], right_view, pre_send.at[2], pre_recv.at[2], across),
-        remote(
-            right_ref.at[1 - cut, 1 - core], right_view, pre_send.at[3], pre_recv.at[3], corner
-        ),
-        remote(right_ref.at[cut, 1 - core], right_view, pre_send.at[4], pre_recv.at[4], partner),
-    )
-    for copy in right_pre:
-        copy.start()
-    left_pair = remote(left_ref, left_view, pre_send.at[5], pre_recv.at[5], partner)
+    left_pair = remote(left_ref, left_view, pre_send.at[2], pre_recv.at[2], partner)
     left_pair.start()
     gram_copy(0).start()
     gram_ref[...] = jnp.zeros_like(gram_ref)
 
     vec_own.wait()
+    for way in range(2):
+        vec_copy(way, 0, core, chip).start()
     vec_pre.wait_recv()
-    for sub in range(2):
-        for way in range(2):
-            vec_copy(way, 0, sub, chip).start()
+    for way in range(2):
+        vec_copy(way, 0, 1 - core, chip).start()
+
+    wide = lax.broadcasted_iota(jnp.int32, (mix_ref.shape[0], slots * pairs), 0)
+    thin = lax.broadcasted_iota(jnp.int32, (mix_ref.shape[0], slots * pairs), 1)
+    stretch = (wide // 8 == thin).astype(jnp.float32)
+    tall = jnp.dot(
+        stretch, square_ref[...],
+        precision=lax.Precision.HIGHEST, preferred_element_type=jnp.float32,
+    )
+    full = lax.dot_general(
+        tall, stretch, (((1,), (1,)), ((), ())),
+        precision=lax.Precision.HIGHEST, preferred_element_type=jnp.float32,
+    )
+    row = lax.broadcasted_iota(jnp.int32, mix_ref.shape, 0)
+    lane = lax.broadcasted_iota(jnp.int32, mix_ref.shape, 1)
+    mix_ref[...] = jnp.where(lax.rem(row, 8) == lax.rem(lane, 8), full, 0.0)
 
     def gram_unit(unit):
         slot = lax.rem(unit, 2)
@@ -395,15 +427,16 @@
         def _():
             gram_unit(index)
 
-    right_own.wait()
+    for copy in right_own:
+        copy.wait()
     for copy in right_pre:
         copy.wait_recv()
     for sub in range(2):
         for way in range(2):
-            right_copy(way, 0, sub, chip).start()
+            right_copy(way, 0, lax.rem(sub + core, 2), chip).start()
 
     left_across.wait_recv()
-    left_pass = remote(left_other, left_other, pre_send.at[6], pre_recv.at[6], partner)
+    left_pass = remote(left_other, left_other, pre_send.at[3], pre_recv.at[3], partner)
     left_pass.start()
 
     @pl.loop(polls - 2, polls)
@@ -476,29 +509,47 @@
             cut_send.at[unit, way], cut_recv.at[piece], across,
         )
 
-    def image_unit(unit):
-        @pl.when(unit >= 2)
+    def image_half(unit, sub):
+        @pl.when((unit >= 2) & (sub == 0))
         def _():
             pair_copy(unit - 2).wait_send()
+
+        at = lax.rem(sub + core, 2)
+        cols = pl.ds(pl.multiple_of(at * span, span), span)
 
         @pl.loop(0, 2)
         def _(k):
             owner = lax.rem(core + 1 + k, 2)
             to = (1 - k) * (chips + lax.rem(unit, 2)) + k * unit
             lines = jnp.concatenate(
-                [right[block_of(unit, way), way * rows : (way + 1) * rows, :] for way in range(2)],
+                [
+                    right[block_of(unit, way), way * rows : (way + 1) * rows, cols]
+                    for way in range(2)
+                ],
                 axis=0,
             )
             out = lax.dot_general(
-                mixed[pl.ds(pl.multiple_of(owner * lot, lot), lot), :],
+                mixed[pl.ds(pl.multiple_of(owner * lot, lot), lot), cols],
                 lines,
                 (((1,), (1,)), ((), ())),
                 preferred_element_type=jnp.float32,
             )
-            for way in range(2):
-                parts[to, way] = out[:, way * rows : (way + 1) * rows].reshape(pairs, rows, rows)
-
-        pair_copy(unit).start()
+
+            @pl.when(sub == 0)
+            def _():
+                for way in range(2):
+                    piece = out[:, way * rows : (way + 1) * rows]
+                    parts[to, way] = piece.reshape(pairs, rows, rows)
+
+            @pl.when(sub == 1)
+            def _():
+                for way in range(2):
+                    piece = out[:, way * rows : (way + 1) * rows]
+                    parts[to, way] += piece.reshape(pairs, rows, rows)
+
+        @pl.when(sub == 1)
+        def _():
+            pair_copy(unit).start()
 
     def join_unit(unit):
         pair_copy(unit).wait_recv()
@@ -516,17 +567,18 @@
         mix_unit(index)
 
     def ready(index):
-        return jnp.minimum(2 * (index - mix_units + 1), (index + 1) // 2 + 1)
+        return jnp.minimum(4 * (index - mix_units + 1), index + 3)
 
     @pl.loop(mix_units, polls)
     def _(index):
         poll(right_copy, index)
 
         @pl.loop(ready(index - 1), ready(index))
-        def _(unit):
-            image_unit(unit)
-
-            @pl.when(unit > 0)
+        def _(piece):
+            unit, sub = piece // 2, lax.rem(piece, 2)
+            image_half(unit, sub)
+
+            @pl.when((unit > 0) & (sub == 1))
             def _():
                 join_unit(unit - 1)
 
@@ -569,11 +621,9 @@
     basis_count = basis.shape[0]
     count = basis_count * (basis_count + 1) // 2
     square = table.transpose(1, 2, 0, 3).reshape(slots * pairs, slots * pairs)
-    mix = jnp.kron(square, jnp.eye(8, dtype=jnp.float32))
-    vec = current.reshape(rows, pairs, 2, quarter).transpose(2, 1, 0, 3)
+    vec = current.transpose(1, 0, 2)
     left = left_env.transpose(1, 0, 2)
-    right = right_env.reshape(rows, half_slots, 2, 2, quarter).transpose(2, 3, 0, 1, 4)
-    right = right.reshape(2, 2, rows, half_slots * quarter)
+    right = right_env.transpose(1, 0, 2)
     bf16, f32 = jnp.bfloat16, jnp.float32
     sem = pltpu.SemaphoreType.DMA
     steps = chips - 1
@@ -593,14 +643,15 @@
             pltpu.VMEM((slots, 2 * rows, depth), bf16),
             pltpu.VMEM((chips, 2 * rows, slots * quarter), bf16),
             pltpu.VMEM((2 * pairs * rows, slots * quarter), bf16),
+            pltpu.VMEM((slots * pairs * 8, slots * pairs * 8), f32),
             pltpu.VMEM((pairs, slots, rows // 2, quarter // 2), f32),
             pltpu.VMEM((chips + 2, 2, pairs, rows, rows), f32),
             pltpu.VMEM((chips, 2, pairs, rows, rows), f32),
             pltpu.VMEM((chips, pairs, rows, rows), f32),
             pltpu.VMEM((2, basis_count, rows // 8, pairs, cols), f32),
-            sem((3,)),
-            sem((7,)),
-            sem((7,)),
+            sem((2 + half_slots,)),
+            sem((4 + 3 * half_slots,)),
+            sem((4 + 3 * half_slots,)),
             sem((2, steps, 2)),
             sem((2, steps, 2)),
             sem((2, steps, 2)),
@@ -614,7 +665,7 @@
         compiler_params=pltpu.CompilerParams(
             vmem_limit_bytes=63 * 1024 * 1024, collective_id=1, has_side_effects=True
         ),
-    )(vec, left, right, mix, basis)
+    )(vec, left, right, square, basis)
 
 
 def finish_kernel(

time: 319 us -> 302 us (0.947)
  local copies, waits for them, and re-layouts: 26.5 us -> 15.3 us
  Pallas kernels: 288 us -> 284 us
    reshape x3 -> x1, local copies, waits for them, and re-layouts: 9.56 us -> 0.7 us  [ring_image(): square = table.transpose(1, 2, 0, 3).reshape(slots * pairs, slots * pairs)]
    transpose x0 -> x1, local copies, waits for them, and re-layouts: none -> 6.56 us  [ring_image(): right = right_env.transpose(1, 0, 2)]
    mul x2 -> x0, local copies, waits for them, and re-layouts: 4.78 us -> none  [ring_image(): mix = jnp.kron(square, jnp.eye(8, dtype=jnp.float32))]
    pallas_call x1, Pallas kernels: 270 us -> 265 us  [ring_image(): pl.pallas_call(ring_kernel, name='ring', in_specs=[hbm, hbm, hbm, vmem, h...]
    unnamed x15 -> x12, local copies, waits for them, and re-layouts: 7.91 us -> 5.08 us
where the time goes in v3:
time: 302 us; the launch traced here: 301 us
  Pallas kernels  284 us (94%)
  local copies, waits for them, and re-layouts  15.3 us (5%)
    pallas_call x1, Pallas kernels, ring_image(): pl.pallas_call(ring_kernel, name='ring', in_specs=[hbm, hbm, hbm, vmem, h...  265 us
    pallas_call x1, Pallas kernels, finish(): pl.pallas_call(functools.partial(finish_kernel, blocks, cuts, entries), n...  19.1 us
    transpose x1, local copies, waits for them, and re-layouts, ring_image(): right = right_env.transpose(1, 0, 2)  6.56 us

profile of v3, /device:TPU:0, one launch (start us, length us, event | category | flops | bytes accessed | tf_op | source)
XLA Modules:
  0.0 301.4 jit_solution(17747343263795073651)
XLA Ops:
  0.6 0.0 copy-start
  0.6 6.6 %copy_bitcast_fusion = (bf16[4,128,2048]{2,1,0:T(8,128)(2,1)}, bf16[4,128,2048]{2,1,0:T(8,128)(2,1)}) fusion(bf16[128,4,2048]{2,1,0:T(4,128)(2,1)} %param.8, bf16[128,4,2048]{2,1,0:T(4,128)(2,1)} %param.7), kind=kLoop, calls=%fused_computation.1 | loop fusion | bytes 8388608 | tf_op jit(solution)/shard_map/transpose | solution.py:626
  7.2 0.0 copy-start.3
  7.2 0.0 copy-start.4
  7.2 2.1 slice.13
  9.3 1.3 copy.36
  10.6 0.0 copy-done.3
  10.6 0.0 copy-done.4
  10.6 0.2 convolution_bitcast_fusion.1
  10.8 0.0 copy-done
  10.8 0.2 convolution_bitcast_fusion
  11.0 0.3 copy.19
  11.3 0.7 reshape.19.square_ref
  12.0 265.2 %ring.1 = (f32[128,4,1024]{2,1,0:T(4,128)}, f32[36,4,128]{2,1,0:T(4,128)}) custom-call(bf16[4,128,1024]{2,1,0:T(8,128)(2,1)} %bitcast.32, bf16[4,128,2048]{2,1,0:T(8,128)(2,1)} %get-tuple-element.14.left_ref, bf16[4,128,2048]{2,1,0:T(8,128)(2,1)} %get-tuple-element.13.right_ref, f32[32,32]{1,0:T(8,128)} %reshape.19.square_ref, f32[8,128,4,1024]{3,2,1,0:T(4,128)} %basis_ref.3), custom_call_target="tpu_custom_call" | custom-call | tf_op jit(solution)/shard_map/ring/pallas_call | solution.py:632
  277.8 0.0 copy-start.1
  277.9 1.6 copy-done.1
  279.4 0.0 copy-start.2
  279.4 0.9 copy-done.2
  280.3 19.1 %finish.1 = (f32[128,4,1024]{2,1,0:T(4,128)S(1)}, f32[16,128]{1,0:T(8,128)S(1)}) custom-call(f32[1]{0:T(128)} %bitcast.30.beta_ref, f32[36,4,128]{2,1,0:T(4,128)S(1)} %copy-done.2, f32[128,4,1024]{2,1,0:T(4,128)S(1)} %copy-done.1, f32[8,128,4,1024]{3,2,1,0:T(4,128)} %basis_ref.3), custom_call_target="tpu_custom_call" | custom-call | tf_op jit(solution)/shard_map/finish/pallas_call | solution.py:809
  299.4 0.6 fusion.6
  300.0 1.3 copy.39
  (1 shorter events, 0.0 us)
Async XLA Ops:
  0.6 10.1 %copy-start = (f32[8,8,2,2]{1,3,2,0:T(2,128)S(1)}, f32[8,8,2,2]{1,3,2,0:T(2,128)}, u32[]{:S(2)}) copy-start(f32[8,8,2,2]{1,3,2,0:T(2,128)} %param.10) | copy-start | bytes 3076
  7.2 3.4 %copy-start.3 = (f32[8,8,2,2]{1,3,2,0:T(2,128)S(1)}, f32[8,8,2,2]{1,3,2,0:T(2,128)}, u32[]{:S(2)}) copy-start(f32[8,8,2,2]{1,3,2,0:T(2,128)} %param.9) | copy-start | bytes 3076
  7.2 3.4 %copy-start.4 = (s32[8]{0:T(128)S(1)}, s32[8]{0:T(128)}, u32[]{:S(2)}) copy-start(s32[8]{0:T(128)} %param.11) | copy-start | bytes 100
  277.8 1.6 copy-start.1
  279.4 0.9 copy-start.2

commit v4 on v1

--- a/solution.py
+++ b/solution.py
@@ -237,24 +237,27 @@
 
 
 def ring_kernel(
-    vec_ref, left_ref, right_ref, mix_ref, basis_ref,
-    image_ref, gram_ref,
-    vec, left, right, mixed, proj, parts, pair_in, cut_in, gram_buf,
+    blocks, cuts, entries,
+    beta_ref, vec_ref, left_ref, right_ref, square_ref, basis_ref,
+    next_ref, values_ref,
+    vec, left, right, mixed, mix_ref, proj, parts, pair_in, cut_in, stream,
+    gram_ref, dots_ref, gram_tile, gram_inbox, dots_tile, dots_inbox,
+    gram_send, gram_recv, dots_send, dots_recv,
     own_sem, pre_send, pre_recv, vec_send, vec_recv, right_send, right_recv,
-    pair_send, pair_recv, cut_send, cut_recv, gram_sem,
+    pair_send, pair_recv, cut_send, cut_recv, stream_sem,
 ):
     chips, pairs, chip_rows, quarter = vec.shape
     slots, _, depth = left.shape
     half_slots, rows, _ = left_ref.shape
-    span = right_ref.shape[3]
+    span = half_slots * quarter
     last = chips - 1
     polls = 2 * last
     row_tile, col_tile = proj.shape[2], proj.shape[3]
     col_tiles = quarter // col_tile
     mix_units = (chip_rows // row_tile) * col_tiles
     basis_count = basis_ref.shape[0]
-    gram_rows = gram_buf.shape[2]
-    gram_units = rows // gram_rows
+    lanes = stream.shape[4]
+    pieces = basis_ref.shape[3] // lanes
     half = chips // 2
 
     blk = lax.axis_index("blk")
@@ -298,7 +301,7 @@
         )
 
     def poll(copy_of, index):
-        step, sub = index // 2, lax.rem(index, 2)
+        step, sub = index // 2, lax.rem(index + core, 2)
         for way in range(2):
             at = from_place(way, step)
             copy_of(way, step, sub, at).wait_recv()
@@ -314,97 +317,162 @@
                 copy_of(way, index // 2, lax.rem(index, 2), chip).wait_send()
 
     mine = pl.ds(core * rows, rows)
-    vec_own = pltpu.make_async_copy(vec_ref.at[core], vec.at[chip, :, mine, :], own_sem.at[0])
+    vec_own = pltpu.make_async_copy(vec_ref.at[:, :, pl.ds(core * quarter, quarter)], vec.at[chip, :, mine, :], own_sem.at[0])
     left_view = left.at[pl.ds(cut * half_slots, half_slots), mine, :]
     left_other = left.at[pl.ds((1 - cut) * half_slots, half_slots), mine, :]
     left_own = pltpu.make_async_copy(left_ref, left_view, own_sem.at[1])
-    right_view = right.at[chip, mine, pl.ds(cut * span, span)]
-    right_own = pltpu.make_async_copy(right_ref.at[cut, core], right_view, own_sem.at[2])
+
+    def slot_view(slot):
+        return right.at[chip, mine, pl.ds(cut * span + slot * quarter, quarter)]
+
+    def slot_part(slot, to_cut, to_core):
+        return right_ref.at[slot, :, pl.ds((2 * to_cut + to_core) * quarter, quarter)]
+
+    def vec_part(to_core):
+        return vec_ref.at[:, :, pl.ds(to_core * quarter, quarter)]
+
+    right_own = [
+        pltpu.make_async_copy(slot_part(slot, cut, core), slot_view(slot), own_sem.at[2 + slot])
+        for slot in range(half_slots)
+    ]
     vec_own.start()
     left_own.start()
-    right_own.start()
-
-    def gram_copy(unit):
-        slot = lax.rem(unit, 2)
+    for copy in right_own:
+        copy.start()
+
+    def stream_copy(piece, slot):
         return pltpu.make_async_copy(
-            basis_ref.at[:, pl.ds(unit * gram_rows, gram_rows), :, :],
-            gram_buf.at[slot],
-            gram_sem.at[slot],
+            basis_ref.at[:, :, :, pl.ds(pl.multiple_of(piece * lanes, lanes), lanes)],
+            stream.at[slot],
+            stream_sem.at[slot],
         )
 
+    devices = blocks * cuts
+    me = blk * cuts + cut
+
+    def place_of(offset):
+        device = lax.rem(me + offset, devices)
+        return (device // cuts, lax.rem(device, cuts))
+
     barrier = pltpu.get_barrier_semaphore()
-    friends = (after, before, partner, across, corner)
-    for friend in friends:
-        pl.semaphore_signal(barrier, inc=1, device_id=friend, device_id_type=MESH)
-    pl.semaphore_wait(barrier, len(friends))
+    for offset in range(1, devices):
+        pl.semaphore_signal(barrier, inc=1, device_id=place_of(offset), device_id_type=MESH)
+    pl.semaphore_wait(barrier, devices - 1)
 
     vec_pre = remote(
-        vec_ref.at[1 - core], vec.at[chip, :, mine, :], pre_send.at[0], pre_recv.at[0], partner
+        vec_part(1 - core), vec.at[chip, :, mine, :], pre_send.at[0], pre_recv.at[0], partner
     )
     vec_pre.start()
+    right_pre = []
+    for way, (to_cut, to_core, device) in enumerate((
+        (1 - cut, core, across), (1 - cut, 1 - core, corner), (cut, 1 - core, partner)
+    )):
+        for slot in range(half_slots):
+            index = 4 + way * half_slots + slot
+            right_pre.append(remote(
+                slot_part(slot, to_cut, to_core), slot_view(slot),
+                pre_send.at[index], pre_recv.at[index], device,
+            ))
+    for copy in right_pre:
+        copy.start()
     left_across = remote(left_ref, left_view, pre_send.at[1], pre_recv.at[1], across)
     left_across.start()
-    right_pre = (
-        remote(right_ref.at[1 - cut, core], right_view, pre_send.at[2], pre_recv.at[2], across),
-        remote(
-            right_ref.at[1 - cut, 1 - core], right_view, pre_send.at[3], pre_recv.at[3], corner
-        ),
-        remote(right_ref.at[cut, 1 - core], right_view, pre_send.at[4], pre_recv.at[4], partner),
-    )
-    for copy in right_pre:
-        copy.start()
-    left_pair = remote(left_ref, left_view, pre_send.at[5], pre_recv.at[5], partner)
+    left_pair = remote(left_ref, left_view, pre_send.at[2], pre_recv.at[2], partner)
     left_pair.start()
-    gram_copy(0).start()
+    stream_copy(0, 0).start()
     gram_ref[...] = jnp.zeros_like(gram_ref)
+    dots_ref[...] = jnp.zeros_like(dots_ref)
 
     vec_own.wait()
+    for way in range(2):
+        vec_copy(way, 0, core, chip).start()
     vec_pre.wait_recv()
-    for sub in range(2):
-        for way in range(2):
-            vec_copy(way, 0, sub, chip).start()
+    for way in range(2):
+        vec_copy(way, 0, 1 - core, chip).start()
+
+    wide = lax.broadcasted_iota(jnp.int32, (mix_ref.shape[0], slots * pairs), 0)
+    thin = lax.broadcasted_iota(jnp.int32, (mix_ref.shape[0], slots * pairs), 1)
+    stretch = (wide // 8 == thin).astype(jnp.float32)
+    tall = jnp.dot(
+        stretch, square_ref[...],
+        precision=lax.Precision.HIGHEST, preferred_element_type=jnp.float32,
+    )
+    full = lax.dot_general(
+        tall, stretch, (((1,), (1,)), ((), ())),
+        precision=lax.Precision.HIGHEST, preferred_element_type=jnp.float32,
+    )
+    row = lax.broadcasted_iota(jnp.int32, mix_ref.shape, 0)
+    lane = lax.broadcasted_iota(jnp.int32, mix_ref.shape, 1)
+    mix_ref[...] = jnp.where(lax.rem(row, 8) == lax.rem(lane, 8), full, 0.0)
 
     def gram_unit(unit):
         slot = lax.rem(unit, 2)
-        gram_copy(unit).wait()
-
-        @pl.when(unit + 1 < gram_units)
+        stream_copy(unit, slot).wait()
+
+        @pl.when(unit + 1 < pieces)
         def _():
-            gram_copy(unit + 1).start()
+            stream_copy(unit + 1, 1 - slot).start()
 
         chunk = 4
 
-        @pl.loop(0, gram_rows // chunk)
+        @pl.loop(0, rows // chunk)
         def _(r):
-            for c in range(gram_buf.shape[4] // 128):
-                vecs = [
-                    gram_buf[slot, j, pl.ds(r * chunk, chunk), :, c * 128 : (c + 1) * 128]
-                    for j in range(basis_count)
-                ]
-                i = 0
-                for j in range(basis_count):
-                    for k in range(j, basis_count):
-                        gram_ref[i] += jnp.sum(vecs[j] * vecs[k], axis=0)
-                        i += 1
+            vecs = [stream[slot, j, pl.ds(r * chunk, chunk), :, :] for j in range(basis_count)]
+            i = 0
+            for j in range(basis_count):
+                for k in range(j, basis_count):
+                    gram_ref[i] += jnp.sum(vecs[j] * vecs[k], axis=0)
+                    i += 1
 
     @pl.loop(0, polls - 2)
     def _(index):
         poll(vec_copy, index)
 
-        @pl.when(index < gram_units)
+        @pl.when(index < pieces)
         def _():
             gram_unit(index)
 
-    right_own.wait()
+    for copy in right_own:
+        copy.wait()
     for copy in right_pre:
         copy.wait_recv()
     for sub in range(2):
         for way in range(2):
-            right_copy(way, 0, sub, chip).start()
+            right_copy(way, 0, lax.rem(sub + core, 2), chip).start()
 
     left_across.wait_recv()
-    left_pass = remote(left_other, left_other, pre_send.at[6], pre_recv.at[6], partner)
+    left_pass = remote(left_other, left_other, pre_send.at[3], pre_recv.at[3], partner)
     left_pass.start()
+
+    def total_of(x):
+        return jnp.sum(jnp.sum(x, axis=0, keepdims=True), axis=1, keepdims=True)
+
+    row = lax.broadcasted_iota(jnp.int32, gram_tile.shape, 0)
+    lane = lax.broadcasted_iota(jnp.int32, gram_tile.shape, 1)
+    found = jnp.zeros(gram_tile.shape, jnp.float32)
+    i = 0
+    for j in range(basis_count):
+        for k in range(j, basis_count):
+            here = ((row == j) & (lane == k)) | ((row == k) & (lane == j))
+            found = jnp.where(here, total_of(gram_ref[i]), found)
+            i += 1
+    gram_tile[...] = found
+    gram_inbox[me] = found
+
+    def gram_copy(offset):
+        return remote(
+            gram_tile, gram_inbox.at[me],
+            gram_send.at[offset], gram_recv.at[offset], place_of(offset),
+        )
+
+    def dots_copy(offset):
+        return remote(
+            dots_tile, dots_inbox.at[me],
+            dots_send.at[offset], dots_recv.at[offset], place_of(offset),
+        )
+
+    for offset in range(1, devices):
+        gram_copy(offset).start()
 
     @pl.loop(polls - 2, polls)
     def _(index):
@@ -476,77 +544,221 @@
             cut_send.at[unit, way], cut_recv.at[piece], across,
         )
 
-    def image_unit(unit):
-        @pl.when(unit >= 2)
+    def image_half(unit, sub):
+        @pl.when((unit >= 2) & (sub == 0))
         def _():
             pair_copy(unit - 2).wait_send()
+
+        at = lax.rem(sub + core, 2)
+        cols = pl.ds(pl.multiple_of(at * span, span), span)
 
         @pl.loop(0, 2)
         def _(k):
             owner = lax.rem(core + 1 + k, 2)
             to = (1 - k) * (chips + lax.rem(unit, 2)) + k * unit
             lines = jnp.concatenate(
-                [right[block_of(unit, way), way * rows : (way + 1) * rows, :] for way in range(2)],
+                [
+                    right[block_of(unit, way), way * rows : (way + 1) * rows, cols]
+                    for way in range(2)
+                ],
                 axis=0,
             )
             out = lax.dot_general(
-                mixed[pl.ds(pl.multiple_of(owner * lot, lot), lot), :],
+                mixed[pl.ds(pl.multiple_of(owner * lot, lot), lot), cols],
                 lines,
                 (((1,), (1,)), ((), ())),
                 preferred_element_type=jnp.float32,
             )
-            for way in range(2):
-                parts[to, way] = out[:, way * rows : (way + 1) * rows].reshape(pairs, rows, rows)
-
-        pair_copy(unit).start()
+
+            @pl.when(sub == 0)
+            def _():
+                for way in range(2):
+                    piece = out[:, way * rows : (way + 1) * rows]
+                    parts[to, way] = piece.reshape(pairs, rows, rows)
+
+            @pl.when(sub == 1)
+            def _():
+                for way in range(2):
+                    piece = out[:, way * rows : (way + 1) * rows]
+                    parts[to, way] += piece.reshape(pairs, rows, rows)
+
+            @pl.when((sub == 1) & (k == 0))
+            def _():
+                pair_copy(unit).start()
 
     def join_unit(unit):
         pair_copy(unit).wait_recv()
         for way in range(2):
             parts[unit, way] += pair_in[unit, way]
-            home, _ = home_of(unit, way)
+            home, piece = home_of(unit, way)
 
             @pl.when(home != cut)
             def _():
                 cut_copy(unit, way).start()
 
-    @pl.loop(0, mix_units)
+    def fetch_unit(unit):
+        for way in range(2):
+            home, piece = home_of(unit, way)
+
+            @pl.when(home == cut)
+            def _():
+                stream_copy(piece, way).start()
+
+    def settle_unit(unit):
+        for way in range(2):
+            home, piece = home_of(unit, way)
+
+            @pl.when(home == cut)
+            def _():
+                cut_copy(unit, way).wait_recv()
+                cols = pl.ds(pl.multiple_of(piece * rows, rows), rows)
+                whole = parts[unit, way] + cut_in[piece]
+                for p in range(pairs):
+                    next_ref[:, p, cols] = whole[p]
+                stream_copy(piece, way).wait()
+
+                def add(step, sums):
+                    sums = list(sums)
+                    for line in range(16):
+                        at = step * 16 + line
+                        image = next_ref[at, :, cols]
+                        for j in range(basis_count):
+                            sums[j] += stream[way, j, at, :, :] * image
+                        sums[basis_count] += image * image
+                    return tuple(sums)
+
+                sums = lax.fori_loop(
+                    0, rows // 16, add, tuple(dots_ref[j] for j in range(basis_count + 1))
+                )
+                for j in range(basis_count + 1):
+                    dots_ref[j] = sums[j]
+
+    first = polls - chips
+
+    @pl.loop(0, first)
     def _(index):
         poll(right_copy, index)
-        mix_unit(index)
+
+        @pl.loop((mix_units * index) // first, (mix_units * (index + 1)) // first)
+        def _(unit):
+            mix_unit(unit)
 
     def ready(index):
-        return jnp.minimum(2 * (index - mix_units + 1), (index + 1) // 2 + 1)
-
-    @pl.loop(mix_units, polls)
+        return jnp.minimum(2 * (index - first) + 3, index + 3)
+
+    @pl.loop(first, polls)
     def _(index):
         poll(right_copy, index)
 
-        @pl.loop(ready(index - 1), ready(index))
-        def _(unit):
-            image_unit(unit)
-
-            @pl.when(unit > 0)
-            def _():
-                join_unit(unit - 1)
-
-    join_unit(last)
+        @pl.loop(jnp.where(index == first, 0, ready(index - 1)), ready(index))
+        def _(piece):
+            unit, sub = piece // 2, lax.rem(piece, 2)
+            image_half(unit, sub)
+
+            @pl.when(sub == 1)
+            def _():
+                join_unit(unit)
+
+            @pl.when((sub == 1) & (unit == 1))
+            def _():
+                fetch_unit(0)
+
+            @pl.when((sub == 1) & (unit > 1) & (unit < last))
+            def _():
+                settle_unit(unit - 2)
+                fetch_unit(unit - 1)
+
+    slots_held = stream.shape[0]
+    stream_copy(0, slots_held - 1).start()
+    settle_unit(last - 2)
+    fetch_unit(last - 1)
+    settle_unit(last - 1)
+    fetch_unit(last)
+    for offset in range(1, devices):
+        gram_copy(offset).wait_recv()
+    gram = gram_inbox[0]
+    for d in range(1, devices):
+        gram = gram + gram_inbox[d]
+    gram = gram / entries
+    settle_unit(last)
+    for piece in range(1, slots_held):
+        stream_copy(piece, piece - 1).start()
+
+    spot = lax.broadcasted_iota(jnp.int32, dots_tile.shape, 1)
+    found = jnp.zeros(dots_tile.shape, jnp.float32)
+    for j in range(basis_count + 1):
+        found = jnp.where(spot == j, total_of(dots_ref[j]), found)
+    dots_tile[...] = found
+    dots_inbox[me] = found
+    for offset in range(1, devices):
+        dots_copy(offset).start()
+    for offset in range(1, devices):
+        dots_copy(offset).wait_recv()
+    along = dots_inbox[0]
+    for d in range(1, devices):
+        along = along + dots_inbox[d]
+    along = along / entries
+
+    n, end, prior = basis_count, basis_count - 1, basis_count - 2
+    spread = jnp.broadcast_to(along, gram_tile.shape)
+    down = jnp.sum(jnp.where(row == lane, spread, 0.0), axis=1, keepdims=True)[0:n]
+    square = along[:, n : n + 1]
+    along = along[:, 0:n]
+    gram = gram[0:n, 0:n]
+    alpha = down[end : end + 1]
+    beta = jnp.full((1, 1), beta_ref[0], jnp.float32)
+    ortho = down - alpha * gram[:, end : end + 1] - beta * gram[:, prior : prior + 1]
+    ortho_row = along - alpha * gram[end : end + 1, :] - beta * gram[prior : prior + 1, :]
+    first = (
+        square
+        - 2.0 * alpha * alpha
+        - 2.0 * beta * down[prior : prior + 1]
+        + alpha * alpha * gram[end : end + 1, end : end + 1]
+        + 2.0 * alpha * beta * gram[end : end + 1, prior : prior + 1]
+        + beta * beta * gram[prior : prior + 1, prior : prior + 1]
+    )
+    bent = jnp.sum(ortho * gram, axis=0, keepdims=True) * ortho_row
+    mean = (
+        first
+        - 2.0 * jnp.sum(ortho * ortho, axis=0, keepdims=True)
+        + jnp.sum(bent, axis=1, keepdims=True)
+    )
+    beta_new = jnp.sqrt(mean + 1e-06)
+    values_ref[...] = jnp.where(
+        (row == 0) & (lane == 0), alpha, jnp.where((row == 0) & (lane == 1), beta_new, 0.0)
+    )
+    index = lax.broadcasted_iota(jnp.int32, ortho.shape, 0)
+    coefs = ortho + jnp.where(index == end, alpha, 0.0) + jnp.where(index == prior, beta, 0.0)
+    coefs = [jnp.broadcast_to(coefs[j : j + 1], (pairs, lanes)) for j in range(n)]
+    scale = jnp.broadcast_to(1.0 / beta_new, (pairs, lanes))
+
+    @pl.loop(0, pieces)
+    def _(piece):
+        slot = lax.rem(piece + slots_held - 1, slots_held)
+        stream_copy(piece, slot).wait()
+        cols = pl.ds(pl.multiple_of(piece * lanes, lanes), lanes)
+
+        @pl.loop(0, rows // 32)
+        def _(step):
+            for line in range(32):
+                at = step * 32 + line
+                value = next_ref[at, :, cols]
+                for j in range(n):
+                    value = value - coefs[j] * stream[slot, j, at, :, :]
+                next_ref[at, :, cols] = value * scale
+
+        @pl.when(piece + slots_held < pieces)
+        def _():
+            stream_copy(piece + slots_held, slot).start()
 
     @pl.loop(0, chips)
     def _(unit):
         for way in range(2):
-            home, piece = home_of(unit, way)
-            copy = cut_copy(unit, way)
-
-            @pl.when(home == cut)
-            def _():
-                copy.wait_recv()
-                cols = pl.ds(pl.multiple_of(piece * rows, rows), rows)
-                image_ref[:, :, cols] = parts[unit, way] + cut_in[piece]
+            home, _ = home_of(unit, way)
 
             @pl.when(home != cut)
             def _():
-                copy.wait_send()
+                cut_copy(unit, way).wait_send()
 
     drain(vec_copy)
     drain(right_copy)
@@ -558,47 +770,61 @@
         copy.wait_send()
     left_pair.wait_send()
     left_pass.wait_send()
-
-
-def ring_image(table, left_env, right_env, current, basis):
+    for offset in range(1, devices):
+        gram_copy(offset).wait_send()
+        dots_copy(offset).wait_send()
+
+
+def ring_step(blocks, cuts, entries, table, left_env, right_env, current, basis, beta_prev):
     rows, half_slots, depth = left_env.shape
     pairs, cols = current.shape[1], current.shape[2]
     slots, chips, quarter = 2 * half_slots, depth // (2 * rows), cols // 2
     basis_count = basis.shape[0]
     count = basis_count * (basis_count + 1) // 2
     square = table.transpose(1, 2, 0, 3).reshape(slots * pairs, slots * pairs)
-    mix = jnp.kron(square, jnp.eye(8, dtype=jnp.float32))
-    vec = current.reshape(rows, pairs, 2, quarter).transpose(2, 1, 0, 3)
+    vec = current.transpose(1, 0, 2)
     left = left_env.transpose(1, 0, 2)
-    right = right_env.reshape(rows, half_slots, 2, 2, quarter).transpose(2, 3, 0, 1, 4)
-    right = right.reshape(2, 2, rows, half_slots * quarter)
+    right = right_env.transpose(1, 0, 2)
     bf16, f32 = jnp.bfloat16, jnp.float32
     sem = pltpu.SemaphoreType.DMA
     steps = chips - 1
     hbm = pl.BlockSpec(memory_space=pltpu.HBM)
     vmem = pl.BlockSpec(memory_space=pltpu.VMEM)
-    return pl.pallas_call(
-        ring_kernel,
+    devices = blocks * cuts
+    smem = pl.BlockSpec(memory_space=pltpu.SMEM)
+    next_vector, values = pl.pallas_call(
+        functools.partial(ring_kernel, blocks, cuts, entries),
         name="ring",
-        in_specs=[hbm, hbm, hbm, vmem, hbm],
+        in_specs=[smem, hbm, hbm, hbm, vmem, hbm],
         out_specs=[vmem, vmem],
         out_shape=[
-            jax.ShapeDtypeStruct((pairs, rows, cols), f32),
-            jax.ShapeDtypeStruct((count, pairs, 128), f32),
+            jax.ShapeDtypeStruct((rows, pairs, cols), f32),
+            jax.ShapeDtypeStruct((8, 128), f32),
         ],
         scratch_shapes=[
             pltpu.VMEM((chips, pairs, 2 * rows, quarter), bf16),
             pltpu.VMEM((slots, 2 * rows, depth), bf16),
             pltpu.VMEM((chips, 2 * rows, slots * quarter), bf16),
             pltpu.VMEM((2 * pairs * rows, slots * quarter), bf16),
+            pltpu.VMEM((slots * pairs * 8, slots * pairs * 8), f32),
             pltpu.VMEM((pairs, slots, rows // 2, quarter // 2), f32),
             pltpu.VMEM((chips + 2, 2, pairs, rows, rows), f32),
             pltpu.VMEM((chips, 2, pairs, rows, rows), f32),
             pltpu.VMEM((chips, pairs, rows, rows), f32),
-            pltpu.VMEM((2, basis_count, rows // 8, pairs, cols), f32),
-            sem((3,)),
-            sem((7,)),
-            sem((7,)),
+            pltpu.VMEM((3, basis_count, rows, pairs, 128), f32),
+            pltpu.VMEM((count, pairs, 128), f32),
+            pltpu.VMEM((basis_count + 1, pairs, 128), f32),
+            pltpu.VMEM((8, 128), f32),
+            pltpu.VMEM((devices, 8, 128), f32),
+            pltpu.VMEM((1, 128), f32),
+            pltpu.VMEM((devices, 1, 128), f32),
+            sem((devices,)),
+            sem((devices,)),
+            sem((devices,)),
+            sem((devices,)),
+            sem((2 + half_slots,)),
+            sem((4 + 3 * half_slots,)),
+            sem((4 + 3 * half_slots,)),
             sem((2, steps, 2)),
             sem((2, steps, 2)),
             sem((2, steps, 2)),
@@ -607,16 +833,17 @@
             sem((chips,)),
             sem((chips, 2)),
             sem((chips,)),
-            sem((2,)),
+            sem((3,)),
         ],
         compiler_params=pltpu.CompilerParams(
-            vmem_limit_bytes=63 * 1024 * 1024, collective_id=1, has_side_effects=True
+            vmem_limit_bytes=65400 * 1024, collective_id=1, has_side_effects=True
         ),
-    )(vec, left, right, mix, basis)
-
-
-def ring_fits(blocks, rows, depth):
-    return blocks == 16 and rows * blocks == depth and rows % 128 == 0
+    )(beta_prev.reshape(1), vec, left, right, square, basis)
+    return next_vector, values[0, 0:1], values[0, 1:2]
+
+
+def ring_fits(blocks, rows, basis_count):
+    return blocks == 16 and rows == 128 and basis_count == 8
 
 
 def gathered_image(cuts, table, left_env, right_env, current):
@@ -665,13 +892,12 @@
     entries = float(full_width * pair_count * full_width)
     table = build_table(left_core, right_core, slot_bond)
     current = krylov_basis[basis_count - 1].astype(jnp.bfloat16)
-    if cuts == 2 and ring_fits(blocks, row_count, full_width):
-        image, gram = ring_image(table, left_env, right_env, current, krylov_basis)
-        image = image.transpose(1, 0, 2)
-        gram = jnp.sum(gram, axis=(1, 2))
-    else:
-        image = gathered_image(cuts, table, left_env, right_env, current)
-        gram = gram_of(krylov_basis)
+    if cuts == 2 and ring_fits(blocks, row_count, basis_count):
+        return ring_step(
+            blocks, cuts, entries, table, left_env, right_env, current, krylov_basis, beta_prev
+        )
+    image = gathered_image(cuts, table, left_env, right_env, current)
+    gram = gram_of(krylov_basis)
 
     sums = lax.psum(jnp.concatenate([gram, dots_of(krylov_basis, image)]), ("blk", "cuts"))
     sums = sums / entries

time: 374 us -> 294 us (0.79)
  blocking collectives: 37.7 us -> 0 us
  local copies, waits for them, and re-layouts: 28.5 us -> 13.3 us
  Pallas kernels: 290 us -> 278 us
  between operations: 9.8 us -> 1.34 us
  other arithmetic: 7.36 us -> 0 us
    psum x1 -> x0, blocking collectives: 37.7 us -> none  [on_device(): lax.psum(jnp.concatenate([gram, dots_of(krylov_basis, image)]), ('blk', '...]
    pallas_call x3 -> x1, Pallas kernels: 290 us -> 278 us  [ring_step(): pl.pallas_call(functools.partial(ring_kernel, blocks, cuts, entries), nam...]
    reshape x4 -> x1, local copies, waits for them, and re-layouts: 9.67 us -> 0.7 us  [ring_step(): square = table.transpose(1, 2, 0, 3).reshape(slots * pairs, slots * pairs)]
    mul x2 -> x0, local copies, waits for them, and re-layouts: 4.78 us -> none  [ring_image(): mix = jnp.kron(square, jnp.eye(8, dtype=jnp.float32))]
    transpose x1 -> x2, local copies, waits for them, and re-layouts: 0.27 us -> 4.6 us  [the longest x1 4.33 us: ring_step(): right = right_env.transpose(1, 0, 2)]
    pallas_call x1 -> x0, local copies, waits for them, and re-layouts: 4.24 us -> none  [ring_image(): pl.pallas_call(ring_kernel, name='ring', in_specs=[hbm, hbm, hbm, vmem, h...]
where the time goes in v4:
time: 294 us; the launch traced here: 293 us
  Pallas kernels  278 us (95%)
  local copies, waits for them, and re-layouts  13.3 us (5%)
    pallas_call x1, Pallas kernels, ring_step(): pl.pallas_call(functools.partial(ring_kernel, blocks, cuts, entries), nam...  278 us

profile of v4, /device:TPU:0, one launch (start us, length us, event | category | flops | bytes accessed | tf_op | source)
XLA Modules:
  0.0 293.4 jit_solution(16659870432659989736)
XLA Ops:
  0.6 0.0 copy-start
  1.3 0.0 copy-done
  1.4 0.9 convolution_bitcast_fusion.1
  2.3 0.2 convolution_bitcast_fusion
  2.5 0.3 copy.19
  2.8 0.7 reshape.19.square_ref
  3.5 0.0 copy-start.1
  3.5 0.0 copy-start.2
  3.5 2.2 slice.13
  5.7 1.3 copy.36
  7.0 0.0 copy-done.1
  7.0 0.0 copy-done.2
  7.0 4.3 %copy_bitcast_fusion = (bf16[4,128,2048]{2,1,0:T(8,128)(2,1)}, bf16[4,128,2048]{2,1,0:T(8,128)(2,1)}) fusion(bf16[128,4,2048]{2,1,0:T(4,128)(2,1)S(1)} %copy-done.1, bf16[128,4,2048]{2,1,0:T(4,128)(2,1)S(1)} %copy-done.2), kind=kLoop, calls=%fused_computation.1 | loop fusion | bytes 8388608 | tf_op jit(solution)/shard_map/transpose | solution.py:787
  11.3 277.7 %ring.1 = (f32[128,4,1024]{2,1,0:T(4,128)}, f32[8,128]{1,0:T(8,128)}) custom-call(f32[1]{0:T(128)} %bitcast.30.beta_ref, bf16[4,128,1024]{2,1,0:T(8,128)(2,1)} %bitcast.32, bf16[4,128,2048]{2,1,0:T(8,128)(2,1)} %get-tuple-element.10.left_ref, bf16[4,128,2048]{2,1,0:T(8,128)(2,1)} %get-tuple-element.9.right_ref, f32[32,32]{1,0:T(8,128)} %reshape.19.square_ref, ...), custom_call_target="tpu_custom_call" | custom-call | tf_op jit(solution)/shard_map/ring/pallas_call | solution.py:795
  289.0 1.3 fusion.6
  290.4 3.1 %copy.39 = f32[128,4,1024]{2,1,0:T(4,128)} copy(f32[128,4,1024]{2,1,0:T(4,128)} %get-tuple-element.14) | data formatting | bytes 4194304
  (1 shorter events, 0.0 us)
Async XLA Ops:
  0.6 0.7 copy-start
  3.5 3.5 %copy-start.1 = (bf16[128,4,2048]{2,1,0:T(4,128)(2,1)S(1)}, bf16[128,4,2048]{2,1,0:T(4,128)(2,1)}, u32[]{:S(2)}) copy-start(bf16[128,4,2048]{2,1,0:T(4,128)(2,1)} %param.8) | copy-start | bytes 6291460
  3.5 3.5 %copy-start.2 = (bf16[128,4,2048]{2,1,0:T(4,128)(2,1)S(1)}, bf16[128,4,2048]{2,1,0:T(4,128)(2,1)}, u32[]{:S(2)}) copy-start(bf16[128,4,2048]{2,1,0:T(4,128)(2,1)} %param.7) | copy-start | bytes 6291460

commit v5 on v4

--- a/solution.py
+++ b/solution.py
@@ -238,17 +238,17 @@
 
 def ring_kernel(
     blocks, cuts, entries,
-    beta_ref, vec_ref, left_ref, right_ref, square_ref, basis_ref,
+    beta_ref, left_ref, right_ref, square_ref, basis_ref,
     next_ref, values_ref,
-    vec, left, right, mixed, mix_ref, proj, parts, pair_in, cut_in, stream,
+    vec, left, right, mixed, mix_ref, proj, parts, pair_in, cut_in, stream, raw,
     gram_ref, dots_ref, gram_tile, gram_inbox, dots_tile, dots_inbox,
     gram_send, gram_recv, dots_send, dots_recv,
-    own_sem, pre_send, pre_recv, vec_send, vec_recv, right_send, right_recv,
+    own_sem, raw_sem, pre_send, pre_recv, vec_send, vec_recv, right_send, right_recv,
     pair_send, pair_recv, cut_send, cut_recv, stream_sem,
 ):
     chips, pairs, chip_rows, quarter = vec.shape
     slots, _, depth = left.shape
-    half_slots, rows, _ = left_ref.shape
+    rows, half_slots, _ = left_ref.shape
     span = half_slots * quarter
     last = chips - 1
     polls = 2 * last
@@ -317,28 +317,21 @@
                 copy_of(way, index // 2, lax.rem(index, 2), chip).wait_send()
 
     mine = pl.ds(core * rows, rows)
-    vec_own = pltpu.make_async_copy(vec_ref.at[:, :, pl.ds(core * quarter, quarter)], vec.at[chip, :, mine, :], own_sem.at[0])
     left_view = left.at[pl.ds(cut * half_slots, half_slots), mine, :]
     left_other = left.at[pl.ds((1 - cut) * half_slots, half_slots), mine, :]
-    left_own = pltpu.make_async_copy(left_ref, left_view, own_sem.at[1])
-
-    def slot_view(slot):
-        return right.at[chip, mine, pl.ds(cut * span + slot * quarter, quarter)]
-
-    def slot_part(slot, to_cut, to_core):
-        return right_ref.at[slot, :, pl.ds((2 * to_cut + to_core) * quarter, quarter)]
-
-    def vec_part(to_core):
-        return vec_ref.at[:, :, pl.ds(to_core * quarter, quarter)]
-
-    right_own = [
-        pltpu.make_async_copy(slot_part(slot, cut, core), slot_view(slot), own_sem.at[2 + slot])
-        for slot in range(half_slots)
-    ]
-    vec_own.start()
-    left_own.start()
-    for copy in right_own:
-        copy.start()
+    right_view = right.at[chip, mine, pl.ds(cut * span, span)]
+    vec_load = pltpu.make_async_copy(basis_ref.at[basis_count - 1], next_ref, own_sem)
+    vec_load.start()
+    raw_rows = raw.shape[1]
+    raw_units = rows // raw_rows
+
+    def raw_copy(unit):
+        source = right_ref if unit < raw_units else left_ref
+        at = pl.ds((unit % raw_units) * raw_rows, raw_rows)
+        return pltpu.make_async_copy(source.at[at], raw.at[unit % 2], raw_sem.at[unit % 2])
+
+    raw_copy(0).start()
+    raw_copy(1).start()
 
     def stream_copy(piece, slot):
         return pltpu.make_async_copy(
@@ -357,38 +350,85 @@
     barrier = pltpu.get_barrier_semaphore()
     for offset in range(1, devices):
         pl.semaphore_signal(barrier, inc=1, device_id=place_of(offset), device_id_type=MESH)
+
+    vec_load.wait()
+    for unit in range(rows // 16):
+        at = slice(unit * 16, (unit + 1) * 16)
+        to = pl.ds(pl.multiple_of(core * rows + unit * 16, 16), 16)
+        for whose in range(2):
+            owner = (core + whose) % 2
+            cols = pl.ds(pl.multiple_of(owner * quarter, quarter), quarter)
+            turned = jnp.swapaxes(next_ref[at, :, cols].astype(vec.dtype), 0, 1)
+            if whose == 0:
+                vec[chip, :, to, :] = turned
+            else:
+                for q in range(pairs):
+                    mixed[at, q * quarter : (q + 1) * quarter] = turned[q]
+
     pl.semaphore_wait(barrier, devices - 1)
 
-    vec_pre = remote(
-        vec_part(1 - core), vec.at[chip, :, mine, :], pre_send.at[0], pre_recv.at[0], partner
-    )
-    vec_pre.start()
-    right_pre = []
-    for way, (to_cut, to_core, device) in enumerate((
-        (1 - cut, core, across), (1 - cut, 1 - core, corner), (cut, 1 - core, partner)
-    )):
-        for slot in range(half_slots):
-            index = 4 + way * half_slots + slot
-            right_pre.append(remote(
-                slot_part(slot, to_cut, to_core), slot_view(slot),
-                pre_send.at[index], pre_recv.at[index], device,
-            ))
+    vec_pre = [
+        remote(
+            mixed.at[pl.ds(0, rows), pl.ds(q * quarter, quarter)], vec.at[chip, q, mine, :],
+            pre_send.at[6 + q], pre_recv.at[6 + q], partner,
+        )
+        for q in range(pairs)
+    ]
+    for copy in vec_pre:
+        copy.start()
+    for way in range(2):
+        vec_copy(way, 0, core, chip).start()
+
+    for unit in range(2 * raw_units):
+        raw_copy(unit).wait()
+        turned = jnp.swapaxes(raw[unit % 2], 0, 1)
+        start = (unit % raw_units) * raw_rows
+        to = pl.ds(pl.multiple_of(core * rows + start, raw_rows), raw_rows)
+        if unit < raw_units:
+            own = pl.ds(pl.multiple_of((2 * cut + core) * quarter, quarter), quarter)
+            owned = jnp.swapaxes(raw[unit % 2, :, :, own], 0, 1)
+            for slot in range(half_slots):
+                cols = pl.ds(pl.multiple_of(cut * span + slot * quarter, quarter), quarter)
+                right[chip, to, cols] = owned[slot]
+                for e in range(4):
+                    at = slice((1 + e) * rows + start, (1 + e) * rows + start + raw_rows)
+                    mixed[at, slot * quarter : (slot + 1) * quarter] = turned[
+                        slot, :, e * quarter : (e + 1) * quarter
+                    ]
+        else:
+            left[pl.ds(cut * half_slots, half_slots), to, :] = turned
+        if unit + 2 < 2 * raw_units:
+            raw_copy(unit + 2).start()
+
+    def right_part(to_cut, to_core):
+        first_row = pl.multiple_of((1 + 2 * to_cut + to_core) * rows, rows)
+        return mixed.at[pl.ds(first_row, rows), pl.ds(0, span)]
+
+    for copy in vec_pre:
+        copy.wait_recv()
+    for way in range(2):
+        vec_copy(way, 0, 1 - core, chip).start()
+
+    right_pre = (
+        remote(
+            right_part(1 - cut, core), right_view, pre_send.at[2], pre_recv.at[2], across
+        ),
+        remote(
+            right_part(1 - cut, 1 - core), right_view, pre_send.at[4], pre_recv.at[4], corner
+        ),
+        remote(
+            right_part(cut, 1 - core), right_view, pre_send.at[5], pre_recv.at[5], partner
+        ),
+    )
     for copy in right_pre:
         copy.start()
-    left_across = remote(left_ref, left_view, pre_send.at[1], pre_recv.at[1], across)
+    left_across = remote(left_view, left_view, pre_send.at[0], pre_recv.at[0], across)
     left_across.start()
-    left_pair = remote(left_ref, left_view, pre_send.at[2], pre_recv.at[2], partner)
+    left_pair = remote(left_view, left_view, pre_send.at[1], pre_recv.at[1], partner)
     left_pair.start()
     stream_copy(0, 0).start()
     gram_ref[...] = jnp.zeros_like(gram_ref)
     dots_ref[...] = jnp.zeros_like(dots_ref)
-
-    vec_own.wait()
-    for way in range(2):
-        vec_copy(way, 0, core, chip).start()
-    vec_pre.wait_recv()
-    for way in range(2):
-        vec_copy(way, 0, 1 - core, chip).start()
 
     wide = lax.broadcasted_iota(jnp.int32, (mix_ref.shape[0], slots * pairs), 0)
     thin = lax.broadcasted_iota(jnp.int32, (mix_ref.shape[0], slots * pairs), 1)
@@ -432,8 +472,6 @@
         def _():
             gram_unit(index)
 
-    for copy in right_own:
-        copy.wait()
     for copy in right_pre:
         copy.wait_recv()
     for sub in range(2):
@@ -478,7 +516,10 @@
     def _(index):
         poll(vec_copy, index)
 
-    left_own.wait()
+    for copy in vec_pre:
+        copy.wait_send()
+    for copy in right_pre:
+        copy.wait_send()
     left_pair.wait_recv()
     left_pass.wait_recv()
 
@@ -526,7 +567,7 @@
 
     def pair_copy(unit):
         return remote(
-            parts.at[chips + lax.rem(unit, 2)], pair_in.at[unit],
+            parts.at[chips + lax.rem(unit, 2)], pair_in.at[lax.rem(unit, 2)],
             pair_send.at[unit], pair_recv.at[unit], partner,
         )
 
@@ -589,7 +630,7 @@
     def join_unit(unit):
         pair_copy(unit).wait_recv()
         for way in range(2):
-            parts[unit, way] += pair_in[unit, way]
+            parts[unit, way] += pair_in[lax.rem(unit, 2), way]
             home, piece = home_of(unit, way)
 
             @pl.when(home != cut)
@@ -764,10 +805,7 @@
     drain(right_copy)
     for unit in (chips - 2, chips - 1):
         pair_copy(unit).wait_send()
-    vec_pre.wait_send()
     left_across.wait_send()
-    for copy in right_pre:
-        copy.wait_send()
     left_pair.wait_send()
     left_pass.wait_send()
     for offset in range(1, devices):
@@ -775,16 +813,13 @@
         dots_copy(offset).wait_send()
 
 
-def ring_step(blocks, cuts, entries, table, left_env, right_env, current, basis, beta_prev):
+def ring_step(blocks, cuts, entries, table, left_env, right_env, basis, beta_prev):
     rows, half_slots, depth = left_env.shape
-    pairs, cols = current.shape[1], current.shape[2]
+    pairs, cols = basis.shape[2], basis.shape[3]
     slots, chips, quarter = 2 * half_slots, depth // (2 * rows), cols // 2
     basis_count = basis.shape[0]
     count = basis_count * (basis_count + 1) // 2
     square = table.transpose(1, 2, 0, 3).reshape(slots * pairs, slots * pairs)
-    vec = current.transpose(1, 0, 2)
-    left = left_env.transpose(1, 0, 2)
-    right = right_env.transpose(1, 0, 2)
     bf16, f32 = jnp.bfloat16, jnp.float32
     sem = pltpu.SemaphoreType.DMA
     steps = chips - 1
@@ -795,7 +830,7 @@
     next_vector, values = pl.pallas_call(
         functools.partial(ring_kernel, blocks, cuts, entries),
         name="ring",
-        in_specs=[smem, hbm, hbm, hbm, vmem, hbm],
+        in_specs=[smem, hbm, hbm, vmem, hbm],
         out_specs=[vmem, vmem],
         out_shape=[
             jax.ShapeDtypeStruct((rows, pairs, cols), f32),
@@ -809,9 +844,10 @@
             pltpu.VMEM((slots * pairs * 8, slots * pairs * 8), f32),
             pltpu.VMEM((pairs, slots, rows // 2, quarter // 2), f32),
             pltpu.VMEM((chips + 2, 2, pairs, rows, rows), f32),
-            pltpu.VMEM((chips, 2, pairs, rows, rows), f32),
+            pltpu.VMEM((2, 2, pairs, rows, rows), f32),
             pltpu.VMEM((chips, pairs, rows, rows), f32),
             pltpu.VMEM((3, basis_count, rows, pairs, 128), f32),
+            pltpu.VMEM((2, 32, half_slots, depth), bf16),
             pltpu.VMEM((count, pairs, 128), f32),
             pltpu.VMEM((basis_count + 1, pairs, 128), f32),
             pltpu.VMEM((8, 128), f32),
@@ -822,9 +858,10 @@
             sem((devices,)),
             sem((devices,)),
             sem((devices,)),
-            sem((2 + half_slots,)),
-            sem((4 + 3 * half_slots,)),
-            sem((4 + 3 * half_slots,)),
+            sem,
+            sem((2,)),
+            sem((6 + pairs,)),
+            sem((6 + pairs,)),
             sem((2, steps, 2)),
             sem((2, steps, 2)),
             sem((2, steps, 2)),
@@ -838,7 +875,7 @@
         compiler_params=pltpu.CompilerParams(
             vmem_limit_bytes=65400 * 1024, collective_id=1, has_side_effects=True
         ),
-    )(beta_prev.reshape(1), vec, left, right, square, basis)
+    )(beta_prev.reshape(1), left_env, right_env, square, basis)
     return next_vector, values[0, 0:1], values[0, 1:2]
 
 
@@ -891,11 +928,11 @@
     full_width = left_env.shape[2]
     entries = float(full_width * pair_count * full_width)
     table = build_table(left_core, right_core, slot_bond)
-    current = krylov_basis[basis_count - 1].astype(jnp.bfloat16)
     if cuts == 2 and ring_fits(blocks, row_count, basis_count):
         return ring_step(
-            blocks, cuts, entries, table, left_env, right_env, current, krylov_basis, beta_prev
-        )
+            blocks, cuts, entries, table, left_env, right_env, krylov_basis, beta_prev
+        )
+    current = krylov_basis[basis_count - 1].astype(jnp.bfloat16)
     image = gathered_image(cuts, table, left_env, right_env, current)
     gram = gram_of(krylov_basis)
 

time: 294 us -> 286 us (0.973)
  local copies, waits for them, and re-layouts: 13.3 us -> 5.41 us
    transpose x1 -> x0, local copies, waits for them, and re-layouts: 4.33 us -> none  [ring_step(): right = right_env.transpose(1, 0, 2)]
where the time goes in v5:
time: 286 us; the launch traced here: 285 us
  Pallas kernels  277 us (97%)
  local copies, waits for them, and re-layouts  5.41 us (2%)
    pallas_call x1, Pallas kernels, ring_step(): pl.pallas_call(functools.partial(ring_kernel, blocks, cuts, entries), nam...  277 us

profile of v5, /device:TPU:0, one launch (start us, length us, event | category | flops | bytes accessed | tf_op | source)
XLA Modules:
  0.0 285.3 jit_solution(12982717430409817087)
XLA Ops:
  0.6 0.0 copy-start
  0.6 0.9 convolution_bitcast_fusion.1
  1.6 0.0 copy-done
  1.6 0.2 convolution_bitcast_fusion
  1.8 0.3 copy.13
  2.1 0.7 reshape.18.square_ref
  3.4 277.5 %ring.1 = (f32[128,4,1024]{2,1,0:T(4,128)}, f32[8,128]{1,0:T(8,128)}) custom-call(f32[1]{0:T(128)} %bitcast.21.beta_ref, bf16[128,4,2048]{2,1,0:T(4,128)(2,1)} %left_ref.1, bf16[128,4,2048]{2,1,0:T(4,128)(2,1)} %right_ref.1, f32[32,32]{1,0:T(8,128)} %reshape.18.square_ref, f32[8,128,4,1024]{3,2,1,0:T(4,128)} %basis_ref.1), custom_call_target="tpu_custom_call" | custom-call | tf_op jit(solution)/shard_map/ring/pallas_call | solution.py:830
  280.9 1.3 fusion.5
  282.3 3.1 %copy.26 = f32[128,4,1024]{2,1,0:T(4,128)} copy(f32[128,4,1024]{2,1,0:T(4,128)} %get-tuple-element.12) | data formatting | bytes 4194304
  (1 shorter events, 0.0 us)
Async XLA Ops:
  0.6 0.9 copy-start

commit v6 on v5

--- a/solution.py
+++ b/solution.py
@@ -285,8 +285,13 @@
             device_id=device, device_id_type=MESH,
         )
 
-    def from_place(way, step):
-        return chip_at(place - 1 - step) if way == 0 else chip_at(place + 1 + step)
+    turn = last - 2
+
+    def off_place(way, off):
+        return chip_at(place - off) if way == 0 else chip_at(place + off)
+
+    def side_of(way, late):
+        return late + way * (1 - 2 * late)
 
     def vec_copy(way, step, sub, at):
         view = vec.at[at, pl.ds(way * (pairs // 2), pairs // 2), pl.ds(sub * rows, rows), :]
@@ -295,20 +300,22 @@
         )
 
     def right_copy(way, step, sub, at):
-        view = right.at[at, pl.ds(way * rows, rows), pl.ds(sub * span, span)]
+        lines = pl.ds(pl.multiple_of(side_of(way, step // turn) * rows, rows), rows)
+        view = right.at[at, lines, pl.ds(sub * span, span)]
         return remote(
             view, view, right_send.at[way, step, sub], right_recv.at[way, step, sub], onward[way]
         )
 
-    def poll(copy_of, index):
+    def poll(copy_of, index, bend):
         step, sub = index // 2, lax.rem(index + core, 2)
         for way in range(2):
-            at = from_place(way, step)
+            at = off_place(way, step + 1 - bend * (step // bend))
             copy_of(way, step, sub, at).wait_recv()
+            bent = (step + 1) // bend - step // bend
 
             @pl.when(step < last - 1)
             def _():
-                copy_of(way, step + 1, sub, at).start()
+                copy_of(way, step + 1, sub, at + bent * (chip - at)).start()
 
     def drain(copy_of):
         @pl.loop(0, polls)
@@ -466,7 +473,7 @@
 
     @pl.loop(0, polls - 2)
     def _(index):
-        poll(vec_copy, index)
+        poll(vec_copy, index, last)
 
         @pl.when(index < pieces)
         def _():
@@ -514,7 +521,7 @@
 
     @pl.loop(polls - 2, polls)
     def _(index):
-        poll(vec_copy, index)
+        poll(vec_copy, index, last)
 
     for copy in vec_pre:
         copy.wait_send()
@@ -571,12 +578,15 @@
             pair_send.at[unit], pair_recv.at[unit], partner,
         )
 
+    def late_of(unit):
+        return unit // (turn + 1)
+
     def block_of(unit, way):
-        return chip_at(place - unit) if way == 0 else chip_at(place + unit)
+        return off_place(way, unit - turn * late_of(unit))
 
     def home_of(unit, way):
         at = block_of(unit, way)
-        return at // half, lax.rem(at, half) * 2 + way
+        return at // half, lax.rem(at, half) * 2 + side_of(way, late_of(unit))
 
     def cut_copy(unit, way):
         _, piece = home_of(unit, way)
@@ -585,6 +595,9 @@
             cut_send.at[unit, way], cut_recv.at[piece], across,
         )
 
+    def lines_of(unit, way):
+        return pl.ds(pl.multiple_of(side_of(way, late_of(unit)) * rows, rows), rows)
+
     def image_half(unit, sub):
         @pl.when((unit >= 2) & (sub == 0))
         def _():
@@ -599,7 +612,7 @@
             to = (1 - k) * (chips + lax.rem(unit, 2)) + k * unit
             lines = jnp.concatenate(
                 [
-                    right[block_of(unit, way), way * rows : (way + 1) * rows, cols]
+                    right[block_of(unit, way), lines_of(unit, way), cols]
                     for way in range(2)
                 ],
                 axis=0,
@@ -678,7 +691,7 @@
 
     @pl.loop(0, first)
     def _(index):
-        poll(right_copy, index)
+        poll(right_copy, index, turn)
 
         @pl.loop((mix_units * index) // first, (mix_units * (index + 1)) // first)
         def _(unit):
@@ -689,7 +702,7 @@
 
     @pl.loop(first, polls)
     def _(index):
-        poll(right_copy, index)
+        poll(right_copy, index, turn)
 
         @pl.loop(jnp.where(index == first, 0, ready(index - 1)), ready(index))
         def _(piece):
@@ -710,7 +723,8 @@
                 fetch_unit(unit - 1)
 
     slots_held = stream.shape[0]
-    stream_copy(0, slots_held - 1).start()
+    for piece in range(slots_held - 2):
+        stream_copy(piece, 2 + piece).start()
     settle_unit(last - 2)
     fetch_unit(last - 1)
     settle_unit(last - 1)
@@ -722,8 +736,8 @@
         gram = gram + gram_inbox[d]
     gram = gram / entries
     settle_unit(last)
-    for piece in range(1, slots_held):
-        stream_copy(piece, piece - 1).start()
+    for slot in range(2):
+        stream_copy(slots_held - 2 + slot, slot).start()
 
     spot = lax.broadcasted_iota(jnp.int32, dots_tile.shape, 1)
     found = jnp.zeros(dots_tile.shape, jnp.float32)
@@ -775,7 +789,7 @@
 
     @pl.loop(0, pieces)
     def _(piece):
-        slot = lax.rem(piece + slots_held - 1, slots_held)
+        slot = lax.rem(piece + 2, slots_held)
         stream_copy(piece, slot).wait()
         cols = pl.ds(pl.multiple_of(piece * lanes, lanes), lanes)
 
@@ -846,7 +860,7 @@
             pltpu.VMEM((chips + 2, 2, pairs, rows, rows), f32),
             pltpu.VMEM((2, 2, pairs, rows, rows), f32),
             pltpu.VMEM((chips, pairs, rows, rows), f32),
-            pltpu.VMEM((3, basis_count, rows, pairs, 128), f32),
+            pltpu.VMEM((4, basis_count, rows, pairs, 128), f32),
             pltpu.VMEM((2, 32, half_slots, depth), bf16),
             pltpu.VMEM((count, pairs, 128), f32),
             pltpu.VMEM((basis_count + 1, pairs, 128), f32),
@@ -870,7 +884,7 @@
             sem((chips,)),
             sem((chips, 2)),
             sem((chips,)),
-            sem((3,)),
+            sem((4,)),
         ],
         compiler_params=pltpu.CompilerParams(
             vmem_limit_bytes=65400 * 1024, collective_id=1, has_side_effects=True

time: 286 us -> 280 us (0.979)
  Pallas kernels: 277 us -> 272 us
    pallas_call x1, Pallas kernels: 277 us -> 272 us  [ring_step(): pl.pallas_call(functools.partial(ring_kernel, blocks, cuts, entries), nam...]
where the time goes in v6:
time: 280 us
  Pallas kernels  272 us (97%)
  local copies, waits for them, and re-layouts  5.41 us (2%)
    pallas_call x1, Pallas kernels, ring_step(): pl.pallas_call(functools.partial(ring_kernel, blocks, cuts, entries), nam...  272 us

profile of v6, /device:TPU:0, one launch (start us, length us, event | category | flops | bytes accessed | tf_op | source)
XLA Modules:
  0.0 279.5 jit_solution(17296727293733987069)
XLA Ops:
  0.6 0.0 copy-start
  0.6 0.9 convolution_bitcast_fusion.1
  1.6 0.0 copy-done
  1.6 0.2 convolution_bitcast_fusion
  1.8 0.3 copy.13
  2.1 0.7 reshape.18.square_ref
  3.4 271.7 %ring.1 = (f32[128,4,1024]{2,1,0:T(4,128)}, f32[8,128]{1,0:T(8,128)}) custom-call(f32[1]{0:T(128)} %bitcast.21.beta_ref, bf16[128,4,2048]{2,1,0:T(4,128)(2,1)} %left_ref.1, bf16[128,4,2048]{2,1,0:T(4,128)(2,1)} %right_ref.1, f32[32,32]{1,0:T(8,128)} %reshape.18.square_ref, f32[8,128,4,1024]{3,2,1,0:T(4,128)} %basis_ref.1), custom_call_target="tpu_custom_call" | custom-call | tf_op jit(solution)/shard_map/ring/pallas_call | solution.py:844
  275.1 1.3 fusion.5
  276.4 3.1 %copy.26 = f32[128,4,1024]{2,1,0:T(4,128)} copy(f32[128,4,1024]{2,1,0:T(4,128)} %get-tuple-element.12) | data formatting | bytes 4194304
  (1 shorter events, 0.0 us)
Async XLA Ops:
  0.6 0.9 copy-start

commit v7 on v6

--- a/solution.py
+++ b/solution.py
@@ -327,8 +327,15 @@
     left_view = left.at[pl.ds(cut * half_slots, half_slots), mine, :]
     left_other = left.at[pl.ds((1 - cut) * half_slots, half_slots), mine, :]
     right_view = right.at[chip, mine, pl.ds(cut * span, span)]
-    vec_load = pltpu.make_async_copy(basis_ref.at[basis_count - 1], next_ref, own_sem)
-    vec_load.start()
+    vec_load = []
+    for part in range(2):
+        at = pl.ds(part * (rows // 2), rows // 2)
+        vec_load.append(
+            pltpu.make_async_copy(
+                basis_ref.at[basis_count - 1, at], next_ref.at[at], own_sem.at[part]
+            )
+        )
+        vec_load[part].start()
     raw_rows = raw.shape[1]
     raw_units = rows // raw_rows
 
@@ -355,24 +362,29 @@
         return (device // cuts, lax.rem(device, cuts))
 
     barrier = pltpu.get_barrier_semaphore()
-    for offset in range(1, devices):
-        pl.semaphore_signal(barrier, inc=1, device_id=place_of(offset), device_id_type=MESH)
-
-    vec_load.wait()
+    friends = (after, before, partner, across, corner)
+    for friend in friends:
+        pl.semaphore_signal(barrier, inc=1, device_id=friend, device_id_type=MESH)
+
+    def turned_vec(unit, owner):
+        at = slice(unit * 16, (unit + 1) * 16)
+        cols = pl.ds(pl.multiple_of(owner * quarter, quarter), quarter)
+        return jnp.swapaxes(next_ref[at, :, cols].astype(vec.dtype), 0, 1)
+
     for unit in range(rows // 16):
-        at = slice(unit * 16, (unit + 1) * 16)
+        if unit % (rows // 32) == 0:
+            vec_load[unit // (rows // 32)].wait()
         to = pl.ds(pl.multiple_of(core * rows + unit * 16, 16), 16)
-        for whose in range(2):
-            owner = (core + whose) % 2
-            cols = pl.ds(pl.multiple_of(owner * quarter, quarter), quarter)
-            turned = jnp.swapaxes(next_ref[at, :, cols].astype(vec.dtype), 0, 1)
-            if whose == 0:
-                vec[chip, :, to, :] = turned
-            else:
-                for q in range(pairs):
-                    mixed[at, q * quarter : (q + 1) * quarter] = turned[q]
-
-    pl.semaphore_wait(barrier, devices - 1)
+        vec[chip, :, to, :] = turned_vec(unit, core)
+
+    pl.semaphore_wait(barrier, len(friends))
+    for way in range(2):
+        vec_copy(way, 0, core, chip).start()
+
+    for unit in range(rows // 16):
+        turned = turned_vec(unit, 1 - core)
+        for q in range(pairs):
+            mixed[unit * 16 : (unit + 1) * 16, q * quarter : (q + 1) * quarter] = turned[q]
 
     vec_pre = [
         remote(
@@ -383,8 +395,6 @@
     ]
     for copy in vec_pre:
         copy.start()
-    for way in range(2):
-        vec_copy(way, 0, core, chip).start()
 
     for unit in range(2 * raw_units):
         raw_copy(unit).wait()
@@ -516,12 +526,12 @@
             dots_send.at[offset], dots_recv.at[offset], place_of(offset),
         )
 
-    for offset in range(1, devices):
-        gram_copy(offset).start()
-
     @pl.loop(polls - 2, polls)
     def _(index):
         poll(vec_copy, index, last)
+
+    for offset in range(1, devices):
+        gram_copy(offset).start()
 
     for copy in vec_pre:
         copy.wait_send()
@@ -872,7 +882,7 @@
             sem((devices,)),
             sem((devices,)),
             sem((devices,)),
-            sem,
+            sem((2,)),
             sem((2,)),
             sem((6 + pairs,)),
             sem((6 + pairs,)),

time: 280 us -> 279 us (level)
  no operation moved by 1% of the time
where the time goes in v7:
time: 279 us; the launch traced here: 278 us
  Pallas kernels  270 us (97%)
  local copies, waits for them, and re-layouts  5.41 us (2%)
    pallas_call x1, Pallas kernels, ring_step(): pl.pallas_call(functools.partial(ring_kernel, blocks, cuts, entries), nam...  270 us

profile of v7, /device:TPU:0, one launch (start us, length us, event | category | flops | bytes accessed | tf_op | source)
XLA Modules:
  0.0 278.3 jit_solution(1256781906904175408)
XLA Ops:
  0.6 0.0 copy-start
  0.6 0.9 convolution_bitcast_fusion.1
  1.6 0.0 copy-done
  1.6 0.2 convolution_bitcast_fusion
  1.8 0.3 copy.13
  2.1 0.7 reshape.18.square_ref
  3.4 270.4 %ring.1 = (f32[128,4,1024]{2,1,0:T(4,128)}, f32[8,128]{1,0:T(8,128)}) custom-call(f32[1]{0:T(128)} %bitcast.21.beta_ref, bf16[128,4,2048]{2,1,0:T(4,128)(2,1)} %left_ref.1, bf16[128,4,2048]{2,1,0:T(4,128)(2,1)} %right_ref.1, f32[32,32]{1,0:T(8,128)} %reshape.18.square_ref, f32[8,128,4,1024]{3,2,1,0:T(4,128)} %basis_ref.1), custom_call_target="tpu_custom_call" | custom-call | tf_op jit(solution)/shard_map/ring/pallas_call | solution.py:854
  273.9 1.3 fusion.5
  275.2 3.1 %copy.26 = f32[128,4,1024]{2,1,0:T(4,128)} copy(f32[128,4,1024]{2,1,0:T(4,128)} %get-tuple-element.12) | data formatting | bytes 4194304
  (1 shorter events, 0.0 us)
Async XLA Ops:
  0.6 0.9 copy-start

commit v8 on v7

--- a/solution.py
+++ b/solution.py
@@ -757,6 +757,26 @@
     dots_inbox[me] = found
     for offset in range(1, devices):
         dots_copy(offset).start()
+
+    @pl.loop(0, chips)
+    def _(unit):
+        for way in range(2):
+            home, _ = home_of(unit, way)
+
+            @pl.when(home != cut)
+            def _():
+                cut_copy(unit, way).wait_send()
+
+    drain(vec_copy)
+    drain(right_copy)
+    for unit in (chips - 2, chips - 1):
+        pair_copy(unit).wait_send()
+    left_across.wait_send()
+    left_pair.wait_send()
+    left_pass.wait_send()
+    for offset in range(1, devices):
+        gram_copy(offset).wait_send()
+
     for offset in range(1, devices):
         dots_copy(offset).wait_recv()
     along = dots_inbox[0]
@@ -816,24 +836,7 @@
         def _():
             stream_copy(piece + slots_held, slot).start()
 
-    @pl.loop(0, chips)
-    def _(unit):
-        for way in range(2):
-            home, _ = home_of(unit, way)
-
-            @pl.when(home != cut)
-            def _():
-                cut_copy(unit, way).wait_send()
-
-    drain(vec_copy)
-    drain(right_copy)
-    for unit in (chips - 2, chips - 1):
-        pair_copy(unit).wait_send()
-    left_across.wait_send()
-    left_pair.wait_send()
-    left_pass.wait_send()
     for offset in range(1, devices):
-        gram_copy(offset).wait_send()
         dots_copy(offset).wait_send()
 
 

time: 279 us -> 278 us (level)
  no operation moved by 1% of the time
where the time goes in v8:
time: 278 us; the launch traced here: 277 us
  Pallas kernels  270 us (97%)
  local copies, waits for them, and re-layouts  5.41 us (2%)
    pallas_call x1, Pallas kernels, ring_step(): pl.pallas_call(functools.partial(ring_kernel, blocks, cuts, entries), nam...  270 us

profile of v8, /device:TPU:0, one launch (start us, length us, event | category | flops | bytes accessed | tf_op | source)
XLA Modules:
  0.0 277.4 jit_solution(3741765479315154766)
XLA Ops:
  0.6 0.0 copy-start
  0.6 0.9 convolution_bitcast_fusion.1
  1.6 0.0 copy-done
  1.6 0.2 convolution_bitcast_fusion
  1.8 0.3 copy.13
  2.1 0.7 reshape.18.square_ref
  3.4 269.5 %ring.1 = (f32[128,4,1024]{2,1,0:T(4,128)}, f32[8,128]{1,0:T(8,128)}) custom-call(f32[1]{0:T(128)} %bitcast.21.beta_ref, bf16[128,4,2048]{2,1,0:T(4,128)(2,1)} %left_ref.1, bf16[128,4,2048]{2,1,0:T(4,128)(2,1)} %right_ref.1, f32[32,32]{1,0:T(8,128)} %reshape.18.square_ref, f32[8,128,4,1024]{3,2,1,0:T(4,128)} %basis_ref.1), custom_call_target="tpu_custom_call" | custom-call | tf_op jit(solution)/shard_map/ring/pallas_call | solution.py:857
  273.0 1.3 fusion.5
  274.3 3.1 %copy.26 = f32[128,4,1024]{2,1,0:T(4,128)} copy(f32[128,4,1024]{2,1,0:T(4,128)} %get-tuple-element.12) | data formatting | bytes 4194304
  (1 shorter events, 0.0 us)
Async XLA Ops:
  0.6 0.9 copy-start
